TPU v7x, 8 devices: a whole 2x2x1 slice. The times are simulated.
8 devices in a mesh: part: 1 (over z), col: 2 (over y), row: 4 (over x, core).
Axes of the slice: x: 2, y: 2, z: 1, core: 2. Of those that a mesh axis runs over, the one named last changes fastest.
Arguments:
- a_blocks: float32 [128, 64, 8192], P(('part', 'row'), None, 'col')
Outputs:
- output: float32 [128, 64, 8192], P(('part', 'row'), None, 'col')
All inputs are finite; a program needn't handle non-finite values.
Results may differ from a plain program's by a relative error of at most 0.001.
Values sent between devices are 32-bit elements.
A program may use at most 1 GiB of HBM per device.

v0:
```python
import jax
import jax.numpy as jnp
from jax import lax
from jax.sharding import PartitionSpec as P

FULL_PRECISION = lax.Precision.HIGHEST


def solution(mesh):
    grid_rows = mesh.shape["row"]
    grid_cols = mesh.shape["col"]

    def local_factor(blocks):
        row_blocks, block_size, local_cols = blocks.shape
        col_blocks = local_cols // block_size
        num_blocks = row_blocks * grid_rows
        my_row = lax.axis_index("row")
        my_col = lax.axis_index("col")
        for k_step in range(num_blocks):
            owner_row = k_step % grid_rows
            owner_col = k_step % grid_cols
            diag_tile = k_step // grid_rows
            diag_lo = (k_step // grid_cols) * block_size
            diag_hi = diag_lo + block_size
            on_row = my_row == owner_row
            on_col = my_col == owner_col
            diag_local = blocks[diag_tile, :, diag_lo:diag_hi]
            diag_sum = lax.psum(jnp.where(on_row, diag_local, 0.0), "row")
            diag_fac = jnp.linalg.cholesky(diag_sum)
            blocks = blocks.at[diag_tile, :, diag_lo:diag_hi].set(jnp.where(on_row & on_col, diag_fac, diag_local))
            row_lo = (k_step + 1) // grid_rows
            if row_lo < row_blocks:
                col_lo = (k_step + 1) // grid_cols
                trail_rows = row_blocks - row_lo
                panel_in = blocks[row_lo:, :, diag_lo:diag_hi]
                solved = lax.linalg.triangular_solve(diag_fac, panel_in.reshape(trail_rows * block_size, block_size), left_side=False, lower=True, transpose_a=True)
                glob_rows = (row_lo + jnp.arange(trail_rows)) * grid_rows + my_row
                keep_rows = (glob_rows > k_step)[:, None, None]
                row_panel = lax.psum(jnp.where(keep_rows & on_col, solved.reshape(trail_rows, block_size, block_size), 0.0), "col")
                blocks = blocks.at[row_lo:, :, diag_lo:diag_hi].set(jnp.where(keep_rows & on_col, row_panel, panel_in))
                gathered = lax.all_gather(row_panel, "row", axis=1).reshape(trail_rows * grid_rows, block_size, block_size)
                padded = jnp.concatenate([jnp.zeros((row_lo * grid_rows, block_size, block_size), blocks.dtype), gathered], axis=0)
                col_panel = lax.dynamic_index_in_dim(padded.reshape(col_blocks, grid_cols, block_size, block_size), my_col, axis=1, keepdims=False)[col_lo:]
                update = lax.dot_general(row_panel.reshape(trail_rows * block_size, block_size), col_panel.reshape((col_blocks - col_lo) * block_size, block_size), (((1,), (1,)), ((), ())), precision=FULL_PRECISION, preferred_element_type=jnp.float32)
                trail_old = blocks[row_lo:, :, col_lo * block_size:]
                blocks = blocks.at[row_lo:, :, col_lo * block_size:].set(trail_old - update.reshape(trail_old.shape))
        shaped = blocks.reshape(row_blocks, block_size, col_blocks, block_size)
        glob_row_ids = (jnp.arange(row_blocks) * grid_rows + my_row)[:, None, None, None]
        glob_col_ids = (jnp.arange(col_blocks) * grid_cols + my_col)[None, None, :, None]
        inner_row = jnp.arange(block_size)[None, :, None, None]
        inner_col = jnp.arange(block_size)[None, None, None, :]
        lower_part = (glob_row_ids > glob_col_ids) | ((glob_row_ids == glob_col_ids) & (inner_row >= inner_col))
        return jnp.where(lower_part, shaped, 0.0).reshape(row_blocks, block_size, local_cols)

    block_spec = P(("part", "row"), None, "col")
    return jax.shard_map(local_factor, mesh=mesh, in_specs=(block_spec,), out_specs=block_spec, check_vma=False)
```

profile of v0, /device:TPU:0, one launch (start us, length us, event | category | flops | bytes accessed | tf_op | source)
XLA Modules:
  0.0 13981.5 jit_solution(5895342685103434203)
XLA Ops:
  6.5 44.2 copy.2157
  170.8 62.4 convolution_subtract_fusion.4
  351.2 74.2 constant_dynamic-update-slice_fusion.261
  547.5 74.4 constant_dynamic-update-slice_fusion.260
  731.7 69.3 constant_dynamic-update-slice_fusion.259
  906.6 69.1 constant_dynamic-update-slice_fusion.257
  1081.5 68.5 constant_dynamic-update-slice_fusion.255
  1256.0 68.5 constant_dynamic-update-slice_fusion.253
  1429.5 66.1 constant_dynamic-update-slice_fusion.251
  1600.8 66.1 constant_dynamic-update-slice_fusion.249
  1771.9 63.9 constant_dynamic-update-slice_fusion.247
  1940.7 63.9 constant_dynamic-update-slice_fusion.245
  2108.8 61.1 constant_dynamic-update-slice_fusion.243
  2273.9 61.1 constant_dynamic-update-slice_fusion.241
  2439.4 61.0 constant_dynamic-update-slice_fusion.239
  2604.7 61.0 constant_dynamic-update-slice_fusion.237
  2768.8 57.7 constant_dynamic-update-slice_fusion.235
  2929.5 57.7 constant_dynamic-update-slice_fusion.233
  3090.5 56.5 constant_dynamic-update-slice_fusion.231
  3250.0 56.5 constant_dynamic-update-slice_fusion.229
  3408.9 54.3 constant_dynamic-update-slice_fusion.227
  3565.3 54.3 constant_dynamic-update-slice_fusion.225
  3721.9 53.6 constant_dynamic-update-slice_fusion.223
  3877.7 53.6 constant_dynamic-update-slice_fusion.221
  4032.8 50.4 constant_dynamic-update-slice_fusion.219
  4184.1 50.4 constant_dynamic-update-slice_fusion.217
  4335.5 49.7 constant_dynamic-update-slice_fusion.215
  4486.4 49.7 constant_dynamic-update-slice_fusion.213
  4636.6 41.9 convolution_subtract_fusion.3
  4806.2 41.9 convolution_subtract_fusion.2
  4975.9 38.1 convolution_subtract_fusion.1
  5141.7 38.1 convolution_subtract_fusion
  5297.5 43.8 constant_dynamic-update-slice_fusion.203
  5431.7 43.8 constant_dynamic-update-slice_fusion.201
  5565.9 44.2 constant_dynamic-update-slice_fusion.199
  5700.4 44.2 constant_dynamic-update-slice_fusion.197
  5834.7 41.7 constant_dynamic-update-slice_fusion.195
  5966.2 41.7 constant_dynamic-update-slice_fusion.193
  6097.7 40.1 constant_dynamic-update-slice_fusion.191
  6227.9 40.1 constant_dynamic-update-slice_fusion.189
  6356.9 38.6 constant_dynamic-update-slice_fusion.187
  6484.3 38.6 constant_dynamic-update-slice_fusion.185
  6611.9 37.7 constant_dynamic-update-slice_fusion.183
  6738.4 37.7 constant_dynamic-update-slice_fusion.181
  6864.1 35.5 constant_dynamic-update-slice_fusion.179
  6987.8 35.4 constant_dynamic-update-slice_fusion.177
  13882.7 43.9 or_select_fusion
  13926.5 48.1 copy.3666
  (3824 shorter events, 11458.8 us)
Async XLA Ops:
  121.8 177.5 %all-reduce.242.cloned.1.call-start = ((), (), s32[]{:S(2)}) async-start(), calls=%async_computation.1 | async-start | bytes 2097152 | tf_op jit(solution)/shard_map/psum | solution.py:39
  302.3 193.2 %all-reduce.244.cloned.1.call-start = ((), (), s32[]{:S(2)}) async-start(), calls=%async_computation.2 | async-start | bytes 2097152 | tf_op jit(solution)/shard_map/psum | solution.py:39
  498.6 193.0 %all-reduce.246.cloned.1.call-start = ((), (), s32[]{:S(2)}) async-start(), calls=%async_computation.3 | async-start | bytes 2031616 | tf_op jit(solution)/shard_map/psum | solution.py:39
  694.6 171.9 %all-reduce.248.cloned.1.call-start = ((), (), s32[]{:S(2)}) async-start(), calls=%async_computation.4 | async-start | bytes 2031616 | tf_op jit(solution)/shard_map/psum | solution.py:39
  869.5 171.9 %all-reduce.250.cloned.1.call-start = ((), (), s32[]{:S(2)}) async-start(), calls=%async_computation.5 | async-start | bytes 2031616 | tf_op jit(solution)/shard_map/psum | solution.py:39
  1044.4 171.5 %all-reduce.252.cloned.1.call-start = ((), (), s32[]{:S(2)}) async-start(), calls=%async_computation.6 | async-start | bytes 2031616 | tf_op jit(solution)/shard_map/psum | solution.py:39
  1218.9 170.5 %all-reduce.254.cloned.1.call-start = ((), (), s32[]{:S(2)}) async-start(), calls=%async_computation.7 | async-start | bytes 1966080 | tf_op jit(solution)/shard_map/psum | solution.py:39
  1392.3 168.3 %all-reduce.256.cloned.1.call-start = ((), (), s32[]{:S(2)}) async-start(), calls=%async_computation.8 | async-start | bytes 1966080 | tf_op jit(solution)/shard_map/psum | solution.py:39
  1563.6 168.1 %all-reduce.258.cloned.1.call-start = ((), (), s32[]{:S(2)}) async-start(), calls=%async_computation.9 | async-start | bytes 1966080 | tf_op jit(solution)/shard_map/psum | solution.py:39
  1734.7 165.9 %all-reduce.260.cloned.1.call-start = ((), (), s32[]{:S(2)}) async-start(), calls=%async_computation.10 | async-start | bytes 1966080 | tf_op jit(solution)/shard_map/psum | solution.py:39
  1903.6 165.3 %all-reduce.262.cloned.1.call-start = ((), (), s32[]{:S(2)}) async-start(), calls=%async_computation.11 | async-start | bytes 1900544 | tf_op jit(solution)/shard_map/psum | solution.py:39
  2071.9 162.1 %all-reduce.264.cloned.1.call-start = ((), (), s32[]{:S(2)}) async-start(), calls=%async_computation.12 | async-start | bytes 1900544 | tf_op jit(solution)/shard_map/psum | solution.py:39
  2237.0 162.4 %all-reduce.266.cloned.1.call-start = ((), (), s32[]{:S(2)}) async-start(), calls=%async_computation.13 | async-start | bytes 1900544 | tf_op jit(solution)/shard_map/psum | solution.py:39
  2402.3 162.4 %all-reduce.268.cloned.1.call-start = ((), (), s32[]{:S(2)}) async-start(), calls=%async_computation.14 | async-start | bytes 1900544 | tf_op jit(solution)/shard_map/psum | solution.py:39
  2567.7 161.3 %all-reduce.270.cloned.1.call-start = ((), (), s32[]{:S(2)}) async-start(), calls=%async_computation.15 | async-start | bytes 1835008 | tf_op jit(solution)/shard_map/psum | solution.py:39
  2731.9 157.8 %all-reduce.272.cloned.1.call-start = ((), (), s32[]{:S(2)}) async-start(), calls=%async_computation.16 | async-start | bytes 1835008 | tf_op jit(solution)/shard_map/psum | solution.py:39
  2892.6 158.0 %all-reduce.274.cloned.1.call-start = ((), (), s32[]{:S(2)}) async-start(), calls=%async_computation.17 | async-start | bytes 1835008 | tf_op jit(solution)/shard_map/psum | solution.py:39
  3053.6 156.6 %all-reduce.276.cloned.1.call-start = ((), (), s32[]{:S(2)}) async-start(), calls=%async_computation.18 | async-start | bytes 1835008 | tf_op jit(solution)/shard_map/psum | solution.py:39
  3213.2 156.0 %all-reduce.278.cloned.1.call-start = ((), (), s32[]{:S(2)}) async-start(), calls=%async_computation.19 | async-start | bytes 1769472 | tf_op jit(solution)/shard_map/psum | solution.py:39
  3372.1 153.5 %all-reduce.280.cloned.1.call-start = ((), (), s32[]{:S(2)}) async-start(), calls=%async_computation.20 | async-start | bytes 1769472 | tf_op jit(solution)/shard_map/psum | solution.py:39
  3528.5 153.7 %all-reduce.282.cloned.1.call-start = ((), (), s32[]{:S(2)}) async-start(), calls=%async_computation.21 | async-start | bytes 1769472 | tf_op jit(solution)/shard_map/psum | solution.py:39
  3685.1 152.8 %all-reduce.284.cloned.1.call-start = ((), (), s32[]{:S(2)}) async-start(), calls=%async_computation.22 | async-start | bytes 1769472 | tf_op jit(solution)/shard_map/psum | solution.py:39
  3840.9 152.3 %all-reduce.286.cloned.1.call-start = ((), (), s32[]{:S(2)}) async-start(), calls=%async_computation.23 | async-start | bytes 1703936 | tf_op jit(solution)/shard_map/psum | solution.py:39
  3996.1 148.4 %all-reduce.288.cloned.1.call-start = ((), (), s32[]{:S(2)}) async-start(), calls=%async_computation.24 | async-start | bytes 1703936 | tf_op jit(solution)/shard_map/psum | solution.py:39
  4147.4 148.4 %all-reduce.290.cloned.1.call-start = ((), (), s32[]{:S(2)}) async-start(), calls=%async_computation.25 | async-start | bytes 1703936 | tf_op jit(solution)/shard_map/psum | solution.py:39
  4298.7 148.0 %all-reduce.292.cloned.1.call-start = ((), (), s32[]{:S(2)}) async-start(), calls=%async_computation.26 | async-start | bytes 1703936 | tf_op jit(solution)/shard_map/psum | solution.py:39
  4449.7 147.4 %all-reduce.294.cloned.1.call-start = ((), (), s32[]{:S(2)}) async-start(), calls=%async_computation.27 | async-start | bytes 1638400 | tf_op jit(solution)/shard_map/psum | solution.py:39
  4600.0 166.7 %all-reduce.296.cloned.1.call-start = ((), (), s32[]{:S(2)}) async-start(), calls=%async_computation.28 | async-start | bytes 1638400 | tf_op jit(solution)/shard_map/psum | solution.py:39
  4769.6 166.7 %all-reduce.298.cloned.1.call-start = ((), (), s32[]{:S(2)}) async-start(), calls=%async_computation.29 | async-start | bytes 1638400 | tf_op jit(solution)/shard_map/psum | solution.py:39
  4939.3 162.9 %all-reduce.300.cloned.1.call-start = ((), (), s32[]{:S(2)}) async-start(), calls=%async_computation.30 | async-start | bytes 1638400 | tf_op jit(solution)/shard_map/psum | solution.py:39
  5105.1 161.1 %all-reduce.302.cloned.1.call-start = ((), (), s32[]{:S(2)}) async-start(), calls=%async_computation.31 | async-start | bytes 1572864 | tf_op jit(solution)/shard_map/psum | solution.py:39
  5268.5 131.9 all-reduce.304.cloned.1.call-start
  5402.7 131.9 all-reduce.306.cloned.1.call-start
  5536.9 132.2 all-reduce.308.cloned.1.call-start
  5671.5 132.0 all-reduce.310.cloned.1.call-start
  5805.8 129.2 all-reduce.312.cloned.1.call-start
  5937.3 129.3 all-reduce.314.cloned.1.call-start
  6068.8 127.9 all-reduce.316.cloned.1.call-start
  6199.0 126.8 all-reduce.318.cloned.1.call-start
  6328.1 125.1 all-reduce.320.cloned.1.call-start
  6455.5 125.3 all-reduce.322.cloned.1.call-start
  6583.1 124.2 all-reduce.324.cloned.1.call-start
  6709.6 123.5 all-reduce.326.cloned.1.call-start
  6835.3 121.4 all-reduce.328.cloned.1.call-start
  6959.0 121.2 all-reduce.330.cloned.1.call-start
  7082.4 120.5 all-reduce.332.cloned.1.call-start
  9518.4 121.4 all-reduce.376.cloned.1.call-start
  9617.1 120.5 all-reduce.378.cloned.1.call-start
  (163 other events, 11081.9 us)
Sparse Core Ops, SparseCore 0:
  84.5 34.3 all-reduce.239
  264.0 35.3 all-reduce.241
  302.4 31.6 all-gather.196
  460.2 35.3 all-reduce.243
  498.7 31.4 all-gather.198
  656.9 34.6 all-reduce.245
  694.7 31.4 all-gather.200
  831.8 34.6 all-reduce.247
  869.6 31.4 all-gather.202
  1006.8 34.6 all-reduce.249
  1044.5 31.4 all-gather.204
  1181.3 34.5 all-reduce.251
  1219.0 31.4 all-gather.206
  1355.4 33.8 all-reduce.253
  1392.5 31.4 all-gather.208
  1526.7 33.8 all-reduce.255
  1563.8 31.4 all-gather.210
  1697.8 33.8 all-reduce.257
  1734.8 31.4 all-gather.212
  1866.7 33.9 all-reduce.259
  1903.7 31.4 all-gather.214
  2035.7 33.1 all-reduce.261
  2072.0 31.4 all-gather.216
  2200.8 33.1 all-reduce.263
  2237.1 31.4 all-gather.218
  2366.1 33.1 all-reduce.265
  2402.5 31.4 all-gather.220
  2531.5 33.1 all-reduce.267
  2567.8 31.4 all-gather.222
  2696.4 32.4 all-reduce.269
  2732.0 31.4 all-gather.224
  2857.2 32.4 all-reduce.271
  2892.8 31.4 all-gather.226
  3018.2 32.4 all-reduce.273
  3053.7 31.4 all-gather.228
  3177.7 32.4 all-reduce.275
  3213.3 31.4 all-gather.230
  3337.4 31.7 all-reduce.277
  3372.2 31.4 all-gather.232
  3493.8 31.7 all-reduce.279
  3528.6 31.4 all-gather.234
  3650.4 31.7 all-reduce.281
  3685.3 31.4 all-gather.236
  3806.2 31.7 all-reduce.283
  3841.0 31.4 all-gather.238
  3996.2 31.4 all-gather.240
  4449.8 31.4 all-gather.246
  4600.1 31.4 all-gather.248
  (134 shorter events, 3195.0 us)
where the time goes:
time: 14000 us
  waiting for transfers between devices  4610 us (33%)
  matrix products  3470 us (25%)
  blocking collectives  2410 us (17%)
  other arithmetic  2280 us (16%)
  local copies, waits for them, and re-layouts  1170 us (8%)
    dot_general x127, matrix products, local_factor(): lax.dot_general(row_panel.reshape(trail_rows * block_size, block_size), c...  3410 us
    psum x115, waiting for transfers between devices, local_factor(): lax.psum(jnp.where(keep_rows & on_col, solved.reshape(trail_rows, block_s...  2900 us
    all_gather x67, waiting for transfers between devices, local_factor(): lax.all_gather(row_panel, 'row', axis=1)  1710 us
    psum x128, blocking collectives, local_factor(): diag_sum = lax.psum(jnp.where(on_row, diag_local, 0.0), 'row')  1350 us
    all_gather x60, blocking collectives, local_factor(): lax.all_gather(row_panel, 'row', axis=1)  957 us
    another operation x384, other arithmetic, local_factor(): diag_fac = jnp.linalg.cholesky(diag_sum)  846 us
    another operation x254, other arithmetic, local_factor(): lax.linalg.triangular_solve(diag_fac, panel_in.reshape(trail_rows * block...  701 us
    unnamed x167, local copies, waits for them, and re-layouts  358 us
  transfers between devices with their start and end apart: 182, of which 182 were waited for; matrix products, arithmetic and copies ran while one was open for 1% of the time, Pallas kernels for 0%

commit v1 on v0

v1 whole, which is shorter than its diff:
```python
import jax
import jax.numpy as jnp
from jax import lax
from jax.experimental import pallas as pl
from jax.experimental.pallas import tpu as pltpu
from jax.sharding import PartitionSpec as P

F32 = jnp.float32
FULL = lax.Precision.HIGHEST
SB = 256
TR = 64
TC = 128
LANES = 128
GROUP = 8
CHUNK = 32
QS = 4
ORDER = (0, 2, 1, 3)


def _nn(a, b):
    return lax.dot_general(a, b, (((1,), (0,)), ((), ())), precision=FULL, preferred_element_type=F32)


def _nt(a, b):
    return lax.dot_general(a, b, (((1,), (1,)), ((), ())), precision=FULL, preferred_element_type=F32)


def _swap_middle(x0, x1):
    low = lax.broadcasted_iota(jnp.int32, x0.shape, 1) < LANES // 2
    half = LANES // 2
    return jnp.where(low, x0, pltpu.roll(x1, half, 1)), jnp.where(low, pltpu.roll(x0, half, 1), x1)


def _factor128(src):
    size = LANES
    lane = lax.broadcasted_iota(jnp.int32, (size, LANES), 1)
    rows = lax.broadcasted_iota(jnp.int32, (size, LANES), 0)
    left = src
    right = jnp.where(lane == rows, 1.0, 0.0).astype(F32)
    rid = lax.broadcasted_iota(jnp.int32, (GROUP, LANES), 0)
    lid = lax.broadcasted_iota(jnp.int32, (GROUP, LANES), 1)
    upper, inverse = [], []
    for g in range(size // GROUP):
        base = GROUP * g
        top_l, top_r = left[:GROUP], right[:GROUP]
        cols = [jnp.broadcast_to(top_l[:, base + j : base + j + 1], (GROUP, LANES)) for j in range(GROUP)]
        scale, row_l, row_r, mult = [], [], [], {}
        for j in range(GROUP):
            inv = lax.rsqrt(cols[j][j : j + 1])
            low = jnp.where(rid > j, cols[j] * inv, 0.0)
            u_l, u_r = top_l[j : j + 1] * inv, top_r[j : j + 1] * inv
            for k in range(j + 1, GROUP):
                mult[j, k] = cols[k][j : j + 1] * inv
                cols[k] = cols[k] - low * mult[j, k]
            top_l = jnp.where(rid == j, u_l, top_l - low * u_l)
            top_r = jnp.where(rid == j, u_r, top_r - low * u_r)
            scale.append(inv)
            row_l.append(u_l)
            row_r.append(u_r)
        upper.append(jnp.where(lid >= rid + base, top_l, 0.0))
        inverse.append(top_r)
        rest = size - base - GROUP
        if rest == 0:
            break
        next_l, next_r = [], []
        for start in range(0, rest, CHUNK):
            stop = min(start + CHUNK, rest)
            a, b = left[GROUP + start : GROUP + stop], right[GROUP + start : GROUP + stop]
            below = [jnp.broadcast_to(a[:, base + j : base + j + 1], (stop - start, LANES)) for j in range(GROUP)]
            for j in range(GROUP):
                low = below[j] * scale[j]
                for k in range(j + 1, GROUP):
                    below[k] = below[k] - low * mult[j, k]
                a = a - low * row_l[j]
                b = b - low * row_r[j]
            next_l.append(a)
            next_r.append(b)
        left = jnp.concatenate(next_l, 0) if len(next_l) > 1 else next_l[0]
        right = jnp.concatenate(next_r, 0) if len(next_r) > 1 else next_r[0]
    return upper, inverse


def _kernel(steps, a_hbm, out_hbm, mat, left, right, xl, xrt, pieces, diag, upper, lower, inv, invp, a1, zeros,
            load_sem, out_sem, sg_send, sg_recv, fw_send, fw_recv, f1_send, f1_recv, f2_send, f2_recv, f3_send, f3_recv):
    r = lax.axis_index("row")
    c = lax.axis_index("col")
    x = r // 2
    p = r % 2
    me = r * 2 + c
    major = p == c
    chunks = steps // QS
    rows, cols = steps * TR, steps * TC
    own = pl.multiple_of(c * TC, TC)
    other = pl.multiple_of((1 - c) * TC, TC)
    y_peer = {"row": r, "col": 1 - c}
    x_peer = {"row": (r + 2) % 4, "col": c}
    z_peer = {"row": (r + 2) % 4, "col": 1 - c}
    d_peer = {"row": 2 * x + 1 - p, "col": c}
    peers = (d_peer, y_peer, x_peer, z_peer)
    xi = (r + 2) % 4

    def small(par, i):
        return pltpu.make_async_remote_copy(pieces.at[par, me], pieces.at[par, me], sg_send.at[par, i],
                                            sg_recv.at[par, i], device_id=peers[i])

    sources = (None, r * 2 + 1 - c, xi * 2 + c, xi * 2 + 1 - c)

    def forward(par, i):
        return pltpu.make_async_remote_copy(pieces.at[par, sources[i]], pieces.at[par, sources[i]], fw_send.at[par, i - 1],
                                            fw_recv.at[par, i - 1], device_id=d_peer)

    def start_small(par):
        for i in range(4):
            small(par, i).start()

    def forward_small(par):
        for i in range(1, 4):
            small(par, i).wait_recv()
            forward(par, i).start()

    def finish_small(par):
        small(par, 0).wait_recv()
        for i in range(1, 4):
            forward(par, i).wait_recv()
        for i in range(4):
            small(par, i).wait_send()
        for i in range(1, 4):
            forward(par, i).wait_send()

    def f1(par, q):
        ref = left.at[par, pl.ds(QS * q, QS), :, pl.ds(own, TC)]
        return pltpu.make_async_remote_copy(ref, ref, f1_send.at[par, q], f1_recv.at[par, q], device_id=y_peer)

    def f2(par, q, h, at):
        return pltpu.make_async_remote_copy(left.at[par, pl.ds(QS * q, QS), :, pl.ds(at, TC)],
                                            right.at[par, pl.ds(QS * q, QS), x, :, pl.ds(at, TC)],
                                            f2_send.at[par, q, h], f2_recv.at[par, q, h], device_id=x_peer)

    def f3a(par, q):
        return pltpu.make_async_remote_copy(left.at[par, pl.ds(QS * q, QS)], right.at[par, pl.ds(QS * q, QS), x],
                                            f3_send.at[par, q, 0], f3_recv.at[par, q, 0], device_id=d_peer)

    def f3b(par, q):
        ref = right.at[par, pl.ds(QS * q, QS), 1 - x]
        return pltpu.make_async_remote_copy(ref, ref, f3_send.at[par, q, 1], f3_recv.at[par, q, 1], device_id=d_peer)

    def rows_of(q):
        return pl.ds(pl.multiple_of(QS * TR * q, QS * TR), QS * TR)

    def cols_of(k, n=1):
        return pl.ds(pl.multiple_of(TC * k, TC), n * TC)

    def each(lo, hi, body):
        def step(i, carry):
            body(i)
            return carry

        lax.fori_loop(lo, hi, step, 0)

    def load(q):
        return pltpu.make_async_copy(a_hbm.at[rows_of(q)], mat.at[rows_of(q)], load_sem.at[q])

    each(0, chunks, lambda q: load(q).start())
    zeros[...] = jnp.zeros_like(zeros)

    def clear(q):
        xl[rows_of(q), :] = jnp.zeros((QS * TR, SB), F32)
        xrt[:, cols_of(QS * q, QS)] = jnp.zeros((SB, QS * TC), F32)

    each(0, chunks, clear)
    each(0, chunks, lambda q: load(q).wait())

    def place_diag(par):
        for i in range(4):
            s0, s1 = _swap_middle(pieces[par, 2 * i, TR:, :], pieces[par, 2 * i + 1, TR:, :])
            diag[TR * i : TR * i + TR, :LANES] = s0
            diag[TR * i : TR * i + TR, LANES:] = s1

    pieces[1, me] = jnp.zeros((2 * TR, TC), F32)
    pieces[1, me, TR:, :] = mat[:TR, :TC]
    start_small(1)
    forward_small(1)
    finish_small(1)
    place_diag(1)

    def relay_one(par, q0):
        def body(q):
            f1(par, q).wait_recv()

            @pl.when(major)
            def _():
                f2(par, q, 1, other).start()
                f3a(par, q).start()
                right[par, pl.ds(QS * q, QS), x] = left[par, pl.ds(QS * q, QS)]

        each(q0, chunks, body)

    def relay_two(par, q0):
        @pl.when(major)
        def _():
            def body(q):
                f2(par, q, 0, own).wait_recv()
                f2(par, q, 1, other).wait_recv()
                f3b(par, q).start()

            each(q0, chunks, body)

    def bulk(k, lo, hi):
        def row_tile(t):
            def tile(u):
                rs = pl.ds(pl.multiple_of(512 * t, 512), 512)
                cs = pl.ds(pl.multiple_of(512 * u, 512), 512)
                mat[rs, cs] = mat[rs, cs] - _nn(xl[rs, :], xrt[:, cs])

            each((k + 2) // 4, 2 * t + 2, tile)

        each(lo, hi, row_tile)

    def step(k, carry):
        par = k % 2
        q0 = k // QS
        more = k < steps - 1
        early = k < steps // 2

        @pl.when(more)
        def _():
            nxt = pl.ds(pl.multiple_of(TR * (k + 1), TR), TR)
            pieces[par, me, :TR, :] = mat[nxt, cols_of(k)]
            pieces[par, me, TR:, :] = mat[nxt, cols_of(k + 1)]
            start_small(par)

            def send(q):
                left[par, pl.ds(QS * q, QS), :, pl.ds(own, TC)] = mat[rows_of(q), cols_of(k)].reshape(QS, TR, TC)
                f1(par, q).start()

                @pl.when(major)
                def _():
                    f2(par, q, 0, own).start()

            each(q0, chunks, send)

        tiles = rows // 512
        first = (k + 2) // 8

        @pl.when(k > 0)
        def _():
            bulk(k, jnp.maximum(first, tiles - 1), tiles)

        @pl.when(more & early)
        def _():
            relay_one(par, q0)

        @pl.when(k > 0)
        def _():
            bulk(k, first, tiles - 1)

        def factor(at):
            u, w = _factor128(diag[at : at + LANES, at : at + LANES])
            for i in range(LANES // GROUP):
                upper[GROUP * i : GROUP * i + GROUP, :] = u[i]
                inv[at + GROUP * i : at + GROUP * i + GROUP, at : at + LANES] = w[i]
            lower[at : at + LANES, at : at + LANES] = upper[...].T

        factor(0)

        @pl.when(more & early)
        def _():
            relay_two(par, q0)

        @pl.when(more & jnp.logical_not(early))
        def _():
            relay_one(par, q0)

        @pl.when(more)
        def _():
            forward_small(par)

        w00 = inv[:LANES, :LANES]
        l10 = _nt(diag[LANES:, :LANES], w00)
        lower[LANES:, :LANES] = l10
        lower[:LANES, LANES:] = jnp.zeros((LANES, LANES), F32)
        diag[LANES:, LANES:] = diag[LANES:, LANES:] - _nt(l10, l10)
        factor(LANES)

        @pl.when(more & jnp.logical_not(early))
        def _():
            relay_two(par, q0)

        inv[LANES:, :LANES] = -_nn(inv[LANES:, LANES:], _nn(l10, w00))
        inv[:LANES, LANES:] = jnp.zeros((LANES, LANES), F32)
        for i in range(4):
            s0, s1 = _swap_middle(inv[TR * ORDER[i] : TR * ORDER[i] + TR, :LANES], inv[TR * ORDER[i] : TR * ORDER[i] + TR, LANES:])
            invp[TR * i : TR * i + TR, :LANES] = s0
            invp[TR * i : TR * i + TR, LANES:] = s1

        @pl.when(more)
        def _():
            finish_small(par)
            for i in range(4):
                a1[TR * i : TR * i + TR, :LANES] = pieces[par, 2 * i, :TR, :]
                a1[TR * i : TR * i + TR, LANES:] = pieces[par, 2 * i + 1, :TR, :]
            place_diag(par)
            x1 = _nt(a1[...], invp[...])
            diag[...] = diag[...] - _nt(x1, x1)

        def put(q):
            return pltpu.make_async_copy(xl.at[rows_of(q), pl.ds(own, TC)], out_hbm.at[rows_of(q), cols_of(k)], out_sem.at[q])

        def put_zero(q, at):
            return pltpu.make_async_copy(zeros, out_hbm.at[rows_of(q), cols_of(at)], out_sem.at[q])

        @pl.when(k > 0)
        def _():
            each(0, chunks, lambda q: put_zero(q, k - 1).wait())

        @pl.when(more)
        def _():
            @pl.when(jnp.logical_not(major))
            def _():
                def body(q):
                    f3a(par, q).wait_recv()
                    f3b(par, q).wait_recv()

                each(q0, chunks, body)

            def solve(q):
                xl[rows_of(q), :] = _nt(left[par, pl.ds(QS * q, QS)].reshape(QS * TR, SB), invp[...])
                xrt[:, cols_of(QS * q, QS)] = _nt(invp[...], right[par, pl.ds(QS * q, QS)].reshape(2 * QS * TR, SB))

            each(q0, chunks, solve)

        def clear_above(i):
            xl[pl.ds(pl.multiple_of(TR * i, TR), TR), :] = jnp.zeros((TR, SB), F32)

        each(QS * q0, k, clear_above)
        mine = pl.ds(pl.multiple_of(TR * r, TR), TR)
        s0, s1 = _swap_middle(lower[mine, :LANES], lower[mine, LANES:])
        at = pl.ds(pl.multiple_of(TR * k, TR), TR)
        xl[at, :LANES] = s0
        xl[at, LANES:] = s1
        each(0, q0, lambda q: put_zero(q, k).start())
        each(q0, chunks, lambda q: put(q).start())

        @pl.when(more)
        def _():
            cs = pl.ds(pl.multiple_of(TC * jnp.minimum(k + 1, steps - 2), TC), 2 * TC)

            def update(q):
                mat[rows_of(q), cs] = mat[rows_of(q), cs] - _nn(xl[rows_of(q), :], xrt[:, cs])

            each((k + 1) // QS, chunks, update)
            xrt[:, cs] = jnp.zeros((SB, 2 * TC), F32)

            def sent(q):
                f1(par, q).wait_send()

                @pl.when(major)
                def _():
                    f2(par, q, 0, own).wait_send()
                    f2(par, q, 1, other).wait_send()
                    f3a(par, q).wait_send()
                    f3b(par, q).wait_send()

            each(q0, chunks, sent)

        return carry

    lax.fori_loop(0, steps, step, 0)
    each(0, chunks, lambda q: pltpu.make_async_copy(zeros, out_hbm.at[rows_of(q), cols_of(steps - 1)], out_sem.at[q]).wait())


def solution(mesh):
    def local_factor(blocks):
        row_blocks, block_size, local_cols = blocks.shape
        rows = row_blocks * block_size
        steps = local_cols // TC
        chunks = steps // QS
        dma = pltpu.SemaphoreType.DMA
        vm = lambda *s: pltpu.VMEM(s, F32)
        out = pl.pallas_call(
            lambda *refs: _kernel(steps, *refs),
            out_shape=jax.ShapeDtypeStruct((rows, local_cols), F32),
            in_specs=[pl.BlockSpec(memory_space=pl.ANY)],
            out_specs=pl.BlockSpec(memory_space=pl.ANY),
            scratch_shapes=[
                vm(rows, local_cols),
                vm(2, steps, TR, SB),
                vm(2, steps, 2, TR, SB),
                vm(rows, SB),
                vm(SB, local_cols),
                vm(2, 8, 2 * TR, TC),
                vm(SB, SB),
                vm(LANES, LANES),
                vm(SB, SB),
                vm(SB, SB),
                vm(SB, SB),
                vm(SB, SB),
                vm(QS * TR, TC),
                dma((chunks,)),
                dma((chunks,)),
                dma((2, 4)),
                dma((2, 4)),
                dma((2, 3)),
                dma((2, 3)),
                dma((2, chunks)),
                dma((2, chunks)),
                dma((2, chunks, 2)),
                dma((2, chunks, 2)),
                dma((2, chunks, 2)),
                dma((2, chunks, 2)),
            ],
            compiler_params=pltpu.CompilerParams(has_side_effects=True, vmem_limit_bytes=67043328),
            name="cholesky",
        )(blocks.reshape(rows, local_cols))
        return out.reshape(row_blocks, block_size, local_cols)

    spec = P(("part", "row"), None, "col")
    return jax.shard_map(local_factor, mesh=mesh, in_specs=(spec,), out_specs=spec, check_vma=False)
```

time: 14000 us -> 1100 us (0.08)
  waiting for transfers between devices: 4610 us -> 0 us
  matrix products: 3470 us -> 0 us
  blocking collectives: 2410 us -> 0 us
  other arithmetic: 2280 us -> 0 us
  local copies, waits for them, and re-layouts: 1170 us -> 23 us
  Pallas kernels: 0 us -> 1080 us
    dot_general x127 -> x0, matrix products: 3410 us -> none  [local_factor(): lax.dot_general(row_panel.reshape(trail_rows * block_size, block_size), c...]
    psum x115 -> x0, waiting for transfers between devices: 2900 us -> none  [local_factor(): lax.psum(jnp.where(keep_rows & on_col, solved.reshape(trail_rows, block_s...]
    all_gather x67 -> x0, waiting for transfers between devices: 1710 us -> none  [local_factor(): lax.all_gather(row_panel, 'row', axis=1)]
    another operation x642 -> x0, other arithmetic: 1560 us -> none  [the longest x384 846 us: local_factor(): diag_fac = jnp.linalg.cholesky(diag_sum)]
    psum x140 -> x0, blocking collectives: 1460 us -> none  [the longest x128 1350 us: local_factor(): diag_sum = lax.psum(jnp.where(on_row, diag_local, 0.0), 'row')]
    pallas_call x0 -> x1, Pallas kernels: none -> 1080 us  [local_factor(): pl.pallas_call(lambda *refs: _kernel(steps, *refs), out_shape=jax.ShapeDt...]
    all_gather x60 -> x0, blocking collectives: 957 us -> none  [local_factor(): lax.all_gather(row_panel, 'row', axis=1)]
    scatter x253 -> x0, other arithmetic: 495 us -> none  [the longest x127 267 us: local_factor(): blocks.at[row_lo:, :, diag_lo:diag_hi]]
  transfers between devices with their start and end apart: 182 -> 0, of which waited for: 182 -> 0; matrix products, arithmetic and copies ran while one was open for 1% -> 0% of each run, Pallas kernels for 0% -> 0%
where the time goes in v1:
time: 1100 us
  Pallas kernels  1080 us (98%)
  local copies, waits for them, and re-layouts  23 us (2%)
    pallas_call x1, Pallas kernels, local_factor(): pl.pallas_call(lambda *refs: _kernel(steps, *refs), out_shape=jax.ShapeDt...  1080 us
    unnamed x1, local copies, waits for them, and re-layouts  23 us

profile of v1, /device:TPU:0, one launch (start us, length us, event | category | flops | bytes accessed | tf_op | source)
XLA Modules:
  0.0 1102.7 jit_solution(6987038280670468921)
XLA Ops:
  0.0 1079.7 %cholesky.1 = f32[2048,4096]{1,0:T(8,128)} custom-call(f32[2048,4096]{1,0:T(8,128)} %bitcast.3), custom_call_target="tpu_custom_call" | custom-call | tf_op jit(solution)/shard_map/cholesky/pallas_call | solution.py:380
  1079.7 23.0 %copy.3 = f32[32,64,4096]{2,1,0:T(8,128)} copy(f32[32,64,4096]{2,1,0:T(8,128)} %bitcast.2) | data formatting | bytes 67108864

commit v2 on v1

v2 whole, which is shorter than its diff:
```python
import jax
import jax.numpy as jnp
from jax import lax
from jax.experimental import pallas as pl
from jax.experimental.pallas import tpu as pltpu
from jax.sharding import PartitionSpec as P

F32 = jnp.float32
FULL = lax.Precision.HIGHEST
SB = 256
TR = 64
TC = 128
LANES = 128
GROUP = 8
CHUNK = 32
QS = 4
WS = 2
TILE = 512
ORDER = (0, 2, 1, 3)


def _nn(a, b):
    return lax.dot_general(a, b, (((1,), (0,)), ((), ())), precision=FULL, preferred_element_type=F32)


def _nt(a, b):
    return lax.dot_general(a, b, (((1,), (1,)), ((), ())), precision=FULL, preferred_element_type=F32)


def _swap_middle(x0, x1):
    low = lax.broadcasted_iota(jnp.int32, x0.shape, 1) < LANES // 2
    half = LANES // 2
    return jnp.where(low, x0, pltpu.roll(x1, half, 1)), jnp.where(low, pltpu.roll(x0, half, 1), x1)


def _factor128(src):
    size = LANES
    lane = lax.broadcasted_iota(jnp.int32, (size, LANES), 1)
    rows = lax.broadcasted_iota(jnp.int32, (size, LANES), 0)
    left = src
    right = jnp.where(lane == rows, 1.0, 0.0).astype(F32)
    rid = lax.broadcasted_iota(jnp.int32, (GROUP, LANES), 0)
    lid = lax.broadcasted_iota(jnp.int32, (GROUP, LANES), 1)
    upper, inverse = [], []
    for g in range(size // GROUP):
        base = GROUP * g
        top_l, top_r = left[:GROUP], right[:GROUP]
        cols = [jnp.broadcast_to(top_l[:, base + j : base + j + 1], (GROUP, LANES)) for j in range(GROUP)]
        scale, row_l, row_r, mult = [], [], [], {}
        for j in range(GROUP):
            inv = lax.rsqrt(cols[j][j : j + 1])
            low = jnp.where(rid > j, cols[j] * inv, 0.0)
            u_l, u_r = top_l[j : j + 1] * inv, top_r[j : j + 1] * inv
            for k in range(j + 1, GROUP):
                mult[j, k] = cols[k][j : j + 1] * inv
                cols[k] = cols[k] - low * mult[j, k]
            top_l = jnp.where(rid == j, u_l, top_l - low * u_l)
            top_r = jnp.where(rid == j, u_r, top_r - low * u_r)
            scale.append(inv)
            row_l.append(u_l)
            row_r.append(u_r)
        upper.append(jnp.where(lid >= rid + base, top_l, 0.0))
        inverse.append(top_r)
        rest = size - base - GROUP
        if rest == 0:
            break
        next_l, next_r = [], []
        for start in range(0, rest, CHUNK):
            stop = min(start + CHUNK, rest)
            a, b = left[GROUP + start : GROUP + stop], right[GROUP + start : GROUP + stop]
            below = [jnp.broadcast_to(a[:, base + j : base + j + 1], (stop - start, LANES)) for j in range(GROUP)]
            for j in range(GROUP):
                low = below[j] * scale[j]
                for k in range(j + 1, GROUP):
                    below[k] = below[k] - low * mult[j, k]
                a = a - low * row_l[j]
                b = b - low * row_r[j]
            next_l.append(a)
            next_r.append(b)
        left = jnp.concatenate(next_l, 0) if len(next_l) > 1 else next_l[0]
        right = jnp.concatenate(next_r, 0) if len(next_r) > 1 else next_r[0]
    return upper, inverse


def _kernel(steps, a_hbm, out_hbm, mat, left, right, xl, xrt, pieces, diag, upper, lower, inv, invp, a1, zeros,
            load_sem, out_sem, sg_send, sg_recv, fw_send, fw_recv, f1_send, f1_recv, f2_send, f2_recv, f3_send, f3_recv):
    r = lax.axis_index("row")
    c = lax.axis_index("col")
    x = r // 2
    p = r % 2
    me = r * 2 + c
    major = p == c
    chunks = steps // QS
    parts = steps // WS
    rows, cols = steps * TR, steps * TC
    tiles = rows // TILE
    own = pl.multiple_of(c * TC, TC)
    other = pl.multiple_of((1 - c) * TC, TC)
    xi = (r + 2) % 4
    y_peer = {"row": r, "col": 1 - c}
    x_peer = {"row": xi, "col": c}
    z_peer = {"row": xi, "col": 1 - c}
    d_peer = {"row": 2 * x + 1 - p, "col": c}
    peers = (d_peer, y_peer, x_peer, z_peer)

    def small(par, i):
        return pltpu.make_async_remote_copy(pieces.at[par, me], pieces.at[par, me], sg_send.at[par, i],
                                            sg_recv.at[par, i], device_id=peers[i])

    sources = (None, r * 2 + 1 - c, xi * 2 + c, xi * 2 + 1 - c)

    def forward(par, i):
        return pltpu.make_async_remote_copy(pieces.at[par, sources[i]], pieces.at[par, sources[i]], fw_send.at[par, i - 1],
                                            fw_recv.at[par, i - 1], device_id=d_peer)

    def start_small(par):
        for i in range(4):
            small(par, i).start()

    def forward_small(par):
        for i in range(1, 4):
            small(par, i).wait_recv()
            forward(par, i).start()

    def finish_small(par):
        small(par, 0).wait_recv()
        for i in range(1, 4):
            forward(par, i).wait_recv()
        for i in range(4):
            small(par, i).wait_send()
        for i in range(1, 4):
            forward(par, i).wait_send()

    def f1(par, w):
        ref = left.at[par, pl.ds(WS * w, WS), :, pl.ds(own, TC)]
        return pltpu.make_async_remote_copy(ref, ref, f1_send.at[par, w], f1_recv.at[par, w], device_id=y_peer)

    def f2(par, w, h, at):
        return pltpu.make_async_remote_copy(left.at[par, pl.ds(WS * w, WS), :, pl.ds(at, TC)],
                                            right.at[par, pl.ds(WS * w, WS), x, :, pl.ds(at, TC)],
                                            f2_send.at[par, w, h], f2_recv.at[par, w, h], device_id=x_peer)

    def f3a(par, w):
        return pltpu.make_async_remote_copy(left.at[par, pl.ds(WS * w, WS)], right.at[par, pl.ds(WS * w, WS), x],
                                            f3_send.at[par, w, 0], f3_recv.at[par, w, 0], device_id=d_peer)

    def f3b(par, w):
        ref = right.at[par, pl.ds(WS * w, WS), 1 - x]
        return pltpu.make_async_remote_copy(ref, ref, f3_send.at[par, w, 1], f3_recv.at[par, w, 1], device_id=d_peer)

    def relay_one(par, w):
        f1(par, w).wait_recv()

        @pl.when(major)
        def _():
            f2(par, w, 1, other).start()
            f3a(par, w).start()
            right[par, pl.ds(WS * w, WS), x] = left[par, pl.ds(WS * w, WS)]

    def relay_two(par, w):
        @pl.when(major)
        def _():
            f2(par, w, 0, own).wait_recv()
            f2(par, w, 1, other).wait_recv()
            f3b(par, w).start()

        @pl.when(jnp.logical_not(major))
        def _():
            f3a(par, w).wait_recv()
            f3b(par, w).wait_recv()

    def sent(par, w):
        f1(par, w).wait_send()

        @pl.when(major)
        def _():
            f2(par, w, 0, own).wait_send()
            f2(par, w, 1, other).wait_send()
            f3a(par, w).wait_send()
            f3b(par, w).wait_send()

    def rows_of(q):
        return pl.ds(pl.multiple_of(QS * TR * q, QS * TR), QS * TR)

    def cols_of(k, n=1):
        return pl.ds(pl.multiple_of(TC * k, TC), n * TC)

    def each(lo, hi, body):
        def step(i, carry):
            body(i)
            return carry

        lax.fori_loop(lo, hi, step, 0)

    head = min(3 * TC, cols)

    def load_head():
        return pltpu.make_async_copy(a_hbm.at[:, pl.ds(0, head)], mat.at[:, pl.ds(0, head)], load_sem.at[chunks])

    def load_rest(q):
        wide = min((QS * TC) * (q + 2), cols) - head
        at = (pl.ds(QS * TR * q, QS * TR), pl.ds(head, wide))
        return pltpu.make_async_copy(a_hbm.at[at], mat.at[at], load_sem.at[q])

    load_head().start()
    for q in range(chunks):
        load_rest(q).start()
    zeros[...] = jnp.zeros_like(zeros)
    load_head().wait()

    def place_diag(par):
        for i in range(4):
            s0, s1 = _swap_middle(pieces[par, 2 * i, TR:, :], pieces[par, 2 * i + 1, TR:, :])
            diag[TR * i : TR * i + TR, :LANES] = s0
            diag[TR * i : TR * i + TR, LANES:] = s1

    pieces[1, me] = jnp.zeros((2 * TR, TC), F32)
    pieces[1, me, TR:, :] = mat[:TR, :TC]
    start_small(1)
    forward_small(1)
    finish_small(1)
    place_diag(1)

    def step(k, carry):
        par = k % 2
        now = k % 3
        last = (k + 2) % 3
        q0 = k // QS
        w0 = (k + 1) // WS
        more = k < steps - 1
        pair = jnp.minimum(k + 1, steps - 2)

        u0 = (k + 2) // QS
        count = 0
        for t in range(tiles):
            count = count + jnp.maximum(2 * t + 2 - u0, 0)
        count = jnp.where(k > 0, count, 0)

        def tile(i):
            t, first, total = 0, 0, 0
            for s in range(tiles):
                total = total + jnp.maximum(2 * s + 2 - u0, 0)
                past = i >= total
                t = t + jnp.where(past, 1, 0)
                first = jnp.where(past, total, first)
            live = i < count
            t = jnp.where(live, t, 0)
            u = jnp.where(live, u0 + i - first, 2 * tiles - 1)
            rs = pl.ds(pl.multiple_of(TILE * t, TILE), TILE)
            cs = pl.ds(pl.multiple_of(TILE * u, TILE), TILE)
            mat[rs, cs] = mat[rs, cs] - _nn(xl[rs, :], xrt[:, cs])

        @pl.when(more)
        def _():
            nxt = pl.ds(pl.multiple_of(TR * (k + 1), TR), TR)
            pieces[par, me, :TR, :] = mat[nxt, cols_of(k)]
            pieces[par, me, TR:, :] = mat[nxt, cols_of(k + 1)]

            def send(w):
                at = pl.ds(pl.multiple_of(WS * TR * w, WS * TR), WS * TR)
                left[now, pl.ds(WS * w, WS), :, pl.ds(own, TC)] = mat[at, cols_of(k)].reshape(WS, TR, TC)
                f1(now, w).start()

                @pl.when(major)
                def _():
                    f2(now, w, 0, own).start()

            send(w0)
            start_small(par)
            each(w0 + 1, parts, send)

        @pl.when(k > 0)
        def _():
            each((k + 1) // WS + 1, parts, lambda w: relay_two(last, w))

            def solve_right(q):
                xrt[:, cols_of(QS * q, QS)] = _nt(invp[1 - par], right[last, pl.ds(QS * q, QS)].reshape(2 * QS * TR, SB))

            each(u0, chunks, solve_right)
            xrt[:, cols_of(jnp.minimum(k, steps - 2), 2)] = jnp.zeros((SB, 2 * TC), F32)

        @pl.when(k == 1)
        def _():
            for q in range(chunks):
                load_rest(q).wait()

        def chain(n):
            def half(h):
                @pl.when(h == 1)
                def _():
                    w00 = inv[:LANES, :LANES]
                    l10 = _nt(diag[LANES:, :LANES], w00)
                    lower[LANES:, :LANES] = l10
                    diag[LANES:, LANES:] = diag[LANES:, LANES:] - _nt(l10, l10)

                span = pl.ds(pl.multiple_of(LANES * h, LANES), LANES)
                for i in range(n):
                    tile(n * h + i)
                u, w = _factor128(diag[span, span])
                for i in range(LANES // GROUP):
                    at = pl.ds(pl.multiple_of(LANES * h + GROUP * i, GROUP), GROUP)
                    upper[GROUP * i : GROUP * i + GROUP, :] = u[i]
                    inv[at, span] = w[i]
                lower[span, span] = upper[...].T

                @pl.when(more & (h == 0))
                def _():
                    relay_one(now, w0)

            each(0, 2, half)

        a_block = jnp.where(count >= 8, 4, jnp.where(count >= 4, 2, 1))
        for n in (4, 2, 1):
            @pl.when(a_block == n)
            def _():
                chain(n)

        @pl.when(more)
        def _():
            forward_small(par)

        inv[LANES:, :LANES] = -_nn(inv[LANES:, LANES:], _nn(lower[LANES:, :LANES], inv[:LANES, :LANES]))
        inv[:LANES, LANES:] = jnp.zeros((LANES, LANES), F32)
        lower[:LANES, LANES:] = jnp.zeros((LANES, LANES), F32)
        for i in range(4):
            s0, s1 = _swap_middle(inv[TR * ORDER[i] : TR * ORDER[i] + TR, :LANES], inv[TR * ORDER[i] : TR * ORDER[i] + TR, LANES:])
            invp[par, TR * i : TR * i + TR, :LANES] = s0
            invp[par, TR * i : TR * i + TR, LANES:] = s1

        many = parts - 1 - w0
        over = jnp.maximum(count - 2 * a_block, 0)

        def share(j):
            return 2 * a_block + (over * j) // jnp.maximum(many, 1)

        def between(j):
            each(share(j), share(j + 1), tile)

            @pl.when(more)
            def _():
                relay_one(now, w0 + 1 + j)

        each(0, jnp.where(more, many, 0), between)
        each(jnp.where(more & (many > 0), count, 2 * a_block), count, tile)

        @pl.when(more)
        def _():
            finish_small(par)
            for i in range(4):
                a1[TR * i : TR * i + TR, :LANES] = pieces[par, 2 * i, :TR, :]
                a1[TR * i : TR * i + TR, LANES:] = pieces[par, 2 * i + 1, :TR, :]
            place_diag(par)
            x1 = _nt(a1[...], invp[par])
            diag[...] = diag[...] - _nt(x1, x1)

        def put(q):
            return pltpu.make_async_copy(xl.at[rows_of(q), pl.ds(own, TC)], out_hbm.at[rows_of(q), cols_of(k)], out_sem.at[q])

        def put_zero(q, at):
            return pltpu.make_async_copy(zeros, out_hbm.at[rows_of(q), cols_of(at)], out_sem.at[q])

        @pl.when(k > 0)
        def _():
            each(0, chunks, lambda q: put_zero(q, k - 1).wait())

        @pl.when(more)
        def _():
            def solve_left(q):
                xl[rows_of(q), :] = _nt(left[now, pl.ds(QS * q, QS)].reshape(QS * TR, SB), invp[par])

            each((k + 1) // QS, chunks, solve_left)
        @pl.when(more)
        def _():
            each(w0, jnp.minimum((k + 2) // WS + 1, parts), lambda w: relay_two(now, w))
            xrt[:, cols_of(pair, 2)] = _nt(invp[par], right[now, pl.ds(pair, 2)].reshape(4 * TR, SB))

        def clear_above(i):
            xl[pl.ds(pl.multiple_of(TR * i, TR), TR), :] = jnp.zeros((TR, SB), F32)

        each(QS * q0, k, clear_above)
        mine = pl.ds(pl.multiple_of(TR * r, TR), TR)
        s0, s1 = _swap_middle(lower[mine, :LANES], lower[mine, LANES:])
        at = pl.ds(pl.multiple_of(TR * k, TR), TR)
        xl[at, :LANES] = s0
        xl[at, LANES:] = s1
        each(0, q0, lambda q: put_zero(q, k).start())
        each(q0, chunks, lambda q: put(q).start())

        @pl.when(more)
        def _():
            cs = cols_of(pair, 2)

            def update(q):
                mat[rows_of(q), cs] = mat[rows_of(q), cs] - _nn(xl[rows_of(q), :], xrt[:, cs])

            each((k + 1) // QS, chunks, update)

        @pl.when(k > 0)
        def _():
            each(k // WS, parts, lambda w: sent(last, w))
        return carry

    lax.fori_loop(0, steps, step, 0)
    each(0, chunks, lambda q: pltpu.make_async_copy(zeros, out_hbm.at[rows_of(q), cols_of(steps - 1)], out_sem.at[q]).wait())


def solution(mesh):
    def local_factor(blocks):
        row_blocks, block_size, local_cols = blocks.shape
        rows = row_blocks * block_size
        steps = local_cols // TC
        chunks, parts = steps // QS, steps // WS
        dma = pltpu.SemaphoreType.DMA
        vm = lambda *s: pltpu.VMEM(s, F32)
        out = pl.pallas_call(
            lambda *refs: _kernel(steps, *refs),
            out_shape=jax.ShapeDtypeStruct((rows, local_cols), F32),
            in_specs=[pl.BlockSpec(memory_space=pl.ANY)],
            out_specs=pl.BlockSpec(memory_space=pl.ANY),
            scratch_shapes=[
                vm(rows, local_cols),
                vm(3, steps, TR, SB),
                vm(3, steps, 2, TR, SB),
                vm(rows, SB),
                vm(SB, local_cols),
                vm(2, 8, 2 * TR, TC),
                vm(SB, SB),
                vm(LANES, LANES),
                vm(SB, SB),
                vm(SB, SB),
                vm(2, SB, SB),
                vm(SB, SB),
                vm(QS * TR, TC),
                dma((chunks + 1,)),
                dma((chunks,)),
                dma((2, 4)),
                dma((2, 4)),
                dma((2, 3)),
                dma((2, 3)),
                dma((3, parts)),
                dma((3, parts)),
                dma((3, parts, 2)),
                dma((3, parts, 2)),
                dma((3, parts, 2)),
                dma((3, parts, 2)),
            ],
            compiler_params=pltpu.CompilerParams(has_side_effects=True, vmem_limit_bytes=67043328),
            name="cholesky",
        )(blocks.reshape(rows, local_cols))
        return out.reshape(row_blocks, block_size, local_cols)

    spec = P(("part", "row"), None, "col")
    return jax.shard_map(local_factor, mesh=mesh, in_specs=(spec,), out_specs=spec, check_vma=False)
```

time: 1100 us -> 780 us (0.71)
  Pallas kernels: 1080 us -> 757 us
    pallas_call x1, Pallas kernels: 1080 us -> 757 us  [local_factor(): pl.pallas_call(lambda *refs: _kernel(steps, *refs), out_shape=jax.ShapeDt...]
where the time goes in v2:
time: 780 us
  Pallas kernels  757 us (97%)
  local copies, waits for them, and re-layouts  23 us (3%)
    pallas_call x1, Pallas kernels, local_factor(): pl.pallas_call(lambda *refs: _kernel(steps, *refs), out_shape=jax.ShapeDt...  757 us
    unnamed x1, local copies, waits for them, and re-layouts  23 us

profile of v2, /device:TPU:0, one launch (start us, length us, event | category | flops | bytes accessed | tf_op | source)
XLA Modules:
  0.0 779.7 jit_solution(10345145872032200742)
XLA Ops:
  0.0 756.7 %cholesky.1 = f32[2048,4096]{1,0:T(8,128)} custom-call(f32[2048,4096]{1,0:T(8,128)} %bitcast.3), custom_call_target="tpu_custom_call" | custom-call | tf_op jit(solution)/shard_map/cholesky/pallas_call | solution.py:415
  756.7 23.0 %copy.3 = f32[32,64,4096]{2,1,0:T(8,128)} copy(f32[32,64,4096]{2,1,0:T(8,128)} %bitcast.2) | data formatting | bytes 67108864

commit v3 on v2

--- a/solution.py
+++ b/solution.py
@@ -15,6 +15,7 @@
 CHUNK = 32
 QS = 4
 WS = 2
+PER = QS // WS
 TILE = 512
 ORDER = (0, 2, 1, 3)
 
@@ -82,7 +83,7 @@
     return upper, inverse
 
 
-def _kernel(steps, a_hbm, out_hbm, mat, left, right, xl, xrt, pieces, diag, upper, lower, inv, invp, a1, zeros,
+def _kernel(steps, a_hbm, out_hbm, mat, left, right, xl, yl, pieces, diag, upper, lower, inv, invp, a1, zeros,
             load_sem, out_sem, sg_send, sg_recv, fw_send, fw_recv, f1_send, f1_recv, f2_send, f2_recv, f3_send, f3_recv):
     r = lax.axis_index("row")
     c = lax.axis_index("col")
@@ -118,12 +119,12 @@
             small(par, i).start()
 
     def forward_small(par):
+        small(par, 0).wait_recv()
         for i in range(1, 4):
             small(par, i).wait_recv()
             forward(par, i).start()
 
     def finish_small(par):
-        small(par, 0).wait_recv()
         for i in range(1, 4):
             forward(par, i).wait_recv()
         for i in range(4):
@@ -157,17 +158,22 @@
             f3a(par, w).start()
             right[par, pl.ds(WS * w, WS), x] = left[par, pl.ds(WS * w, WS)]
 
-    def relay_two(par, w):
+    def pass_on(par, w):
         @pl.when(major)
         def _():
             f2(par, w, 0, own).wait_recv()
             f2(par, w, 1, other).wait_recv()
             f3b(par, w).start()
 
+    def take(par, w):
         @pl.when(jnp.logical_not(major))
         def _():
             f3a(par, w).wait_recv()
             f3b(par, w).wait_recv()
+
+    def relay_two(par, w):
+        pass_on(par, w)
+        take(par, w)
 
     def sent(par, w):
         f1(par, w).wait_send()
@@ -177,7 +183,6 @@
             f2(par, w, 0, own).wait_send()
             f2(par, w, 1, other).wait_send()
             f3a(par, w).wait_send()
-            f3b(par, w).wait_send()
 
     def rows_of(q):
         return pl.ds(pl.multiple_of(QS * TR * q, QS * TR), QS * TR)
@@ -203,10 +208,14 @@
         return pltpu.make_async_copy(a_hbm.at[at], mat.at[at], load_sem.at[q])
 
     load_head().start()
+    barrier = pltpu.get_barrier_semaphore()
+    for peer in peers:
+        pl.semaphore_signal(barrier, inc=1, device_id=peer)
+    zeros[...] = jnp.zeros_like(zeros)
+    load_head().wait()
     for q in range(chunks):
         load_rest(q).start()
-    zeros[...] = jnp.zeros_like(zeros)
-    load_head().wait()
+    pl.semaphore_wait(barrier, len(peers))
 
     def place_diag(par):
         for i in range(4):
@@ -214,21 +223,45 @@
             diag[TR * i : TR * i + TR, :LANES] = s0
             diag[TR * i : TR * i + TR, LANES:] = s1
 
-    pieces[1, me] = jnp.zeros((2 * TR, TC), F32)
-    pieces[1, me, TR:, :] = mat[:TR, :TC]
-    start_small(1)
-    forward_small(1)
-    finish_small(1)
-    place_diag(1)
+    def stage(k, w):
+        slot = k % 3
+        f1(slot, w).start()
+
+        @pl.when(major)
+        def _():
+            f2(slot, w, 0, own).start()
+
+    def stage_small(k):
+        slot = k % 3
+        nxt = pl.ds(pl.multiple_of(TR * (k + 1), TR), TR)
+        pieces[slot, me, :TR, :] = mat[nxt, cols_of(k)]
+        pieces[slot, me, TR:, :] = mat[nxt, cols_of(k + 1)]
+        start_small(slot)
+
+    pieces[2, me, :TR, :] = jnp.zeros((TR, TC), F32)
+    pieces[2, me, TR:, :] = mat[:TR, :TC]
+    start_small(2)
+
+    def first(q):
+        left[0, pl.ds(QS * q, QS), :, pl.ds(own, TC)] = mat[rows_of(q), :TC].reshape(QS, TR, TC)
+
+    each(0, chunks, first)
+    stage(0, 0)
+    stage_small(0)
+    each(1, parts, lambda w: stage(0, w))
+    forward_small(2)
+    finish_small(2)
+    place_diag(2)
 
     def step(k, carry):
-        par = k % 2
         now = k % 3
         last = (k + 2) % 3
         q0 = k // QS
         w0 = (k + 1) // WS
         more = k < steps - 1
         pair = jnp.minimum(k + 1, steps - 2)
+        w1 = jnp.minimum((k + 2) // WS, parts - 1)
+        ahead = w1 + 1
 
         u0 = (k + 2) // QS
         count = 0
@@ -248,36 +281,17 @@
             u = jnp.where(live, u0 + i - first, 2 * tiles - 1)
             rs = pl.ds(pl.multiple_of(TILE * t, TILE), TILE)
             cs = pl.ds(pl.multiple_of(TILE * u, TILE), TILE)
-            mat[rs, cs] = mat[rs, cs] - _nn(xl[rs, :], xrt[:, cs])
-
-        @pl.when(more)
-        def _():
-            nxt = pl.ds(pl.multiple_of(TR * (k + 1), TR), TR)
-            pieces[par, me, :TR, :] = mat[nxt, cols_of(k)]
-            pieces[par, me, TR:, :] = mat[nxt, cols_of(k + 1)]
-
-            def send(w):
-                at = pl.ds(pl.multiple_of(WS * TR * w, WS * TR), WS * TR)
-                left[now, pl.ds(WS * w, WS), :, pl.ds(own, TC)] = mat[at, cols_of(k)].reshape(WS, TR, TC)
-                f1(now, w).start()
-
-                @pl.when(major)
-                def _():
-                    f2(now, w, 0, own).start()
-
-            send(w0)
-            start_small(par)
-            each(w0 + 1, parts, send)
+            mat[rs, cs] = mat[rs, cs] - _nt(yl[rs, :], right[last, pl.ds(QS * u, QS)].reshape(TILE, SB))
 
         @pl.when(k > 0)
         def _():
             each((k + 1) // WS + 1, parts, lambda w: relay_two(last, w))
 
-            def solve_right(q):
-                xrt[:, cols_of(QS * q, QS)] = _nt(invp[1 - par], right[last, pl.ds(QS * q, QS)].reshape(2 * QS * TR, SB))
-
-            each(u0, chunks, solve_right)
-            xrt[:, cols_of(jnp.minimum(k, steps - 2), 2)] = jnp.zeros((SB, 2 * TC), F32)
+            @pl.when(major)
+            def _():
+                each(k // WS, jnp.minimum((k + 1) // WS + 1, parts), lambda w: f3b(last, w).wait_send())
+
+            right[last, pl.ds(jnp.minimum(k, steps - 2), 2)] = jnp.zeros((2, 2, TR, SB), F32)
 
         @pl.when(k == 1)
         def _():
@@ -305,7 +319,8 @@
 
                 @pl.when(more & (h == 0))
                 def _():
-                    relay_one(now, w0)
+                    forward_small(now)
+                    each(w0, ahead, lambda w: relay_one(now, w))
 
             each(0, 2, half)
 
@@ -317,17 +332,23 @@
 
         @pl.when(more)
         def _():
-            forward_small(par)
+            each(w0, w1 + 1, lambda w: pass_on(now, w))
 
         inv[LANES:, :LANES] = -_nn(inv[LANES:, LANES:], _nn(lower[LANES:, :LANES], inv[:LANES, :LANES]))
         inv[:LANES, LANES:] = jnp.zeros((LANES, LANES), F32)
         lower[:LANES, LANES:] = jnp.zeros((LANES, LANES), F32)
         for i in range(4):
             s0, s1 = _swap_middle(inv[TR * ORDER[i] : TR * ORDER[i] + TR, :LANES], inv[TR * ORDER[i] : TR * ORDER[i] + TR, LANES:])
-            invp[par, TR * i : TR * i + TR, :LANES] = s0
-            invp[par, TR * i : TR * i + TR, LANES:] = s1
-
-        many = parts - 1 - w0
+            invp[TR * i : TR * i + TR, :LANES] = s0
+            invp[TR * i : TR * i + TR, LANES:] = s1
+
+        def put(q):
+            return pltpu.make_async_copy(xl.at[rows_of(q), pl.ds(own, TC)], out_hbm.at[rows_of(q), cols_of(k)], out_sem.at[q])
+
+        def put_zero(q, at):
+            return pltpu.make_async_copy(zeros, out_hbm.at[rows_of(q), cols_of(at)], out_sem.at[q])
+
+        many = parts - ahead
         over = jnp.maximum(count - 2 * a_block, 0)
 
         def share(j):
@@ -335,44 +356,70 @@
 
         def between(j):
             each(share(j), share(j + 1), tile)
-
-            @pl.when(more)
-            def _():
-                relay_one(now, w0 + 1 + j)
+            relay_one(now, ahead + j)
 
         each(0, jnp.where(more, many, 0), between)
         each(jnp.where(more & (many > 0), count, 2 * a_block), count, tile)
 
+        @pl.when(k > 0)
+        def _():
+            each(k // WS, parts, lambda w: sent(last, w))
+
+            @pl.when(major)
+            def _():
+                each((k + 1) // WS + 1, parts, lambda w: f3b(last, w).wait_send())
+
+            each(0, chunks, lambda q: put_zero(q, k - 1).wait())
+
+        def chunk_of(q):
+            return left[now, pl.ds(QS * q, QS)].reshape(QS * TR, SB)
+
+        q1 = (k + 1) // QS
+        q2 = jnp.minimum(q1 + 1, chunks - 1)
+
         @pl.when(more)
         def _():
-            finish_small(par)
+            each(w0, w1 + 1, lambda w: take(now, w))
+            finish_small(now)
             for i in range(4):
-                a1[TR * i : TR * i + TR, :LANES] = pieces[par, 2 * i, :TR, :]
-                a1[TR * i : TR * i + TR, LANES:] = pieces[par, 2 * i + 1, :TR, :]
-            place_diag(par)
-            x1 = _nt(a1[...], invp[par])
+                a1[TR * i : TR * i + TR, :LANES] = pieces[now, 2 * i, :TR, :]
+                a1[TR * i : TR * i + TR, LANES:] = pieces[now, 2 * i + 1, :TR, :]
+            place_diag(now)
+            x1 = _nt(a1[...], invp[...])
+            xa = _nt(chunk_of(q1), invp[...])
+            xb = _nt(chunk_of(q2), invp[...])
             diag[...] = diag[...] - _nt(x1, x1)
-
-        def put(q):
-            return pltpu.make_async_copy(xl.at[rows_of(q), pl.ds(own, TC)], out_hbm.at[rows_of(q), cols_of(k)], out_sem.at[q])
-
-        def put_zero(q, at):
-            return pltpu.make_async_copy(zeros, out_hbm.at[rows_of(q), cols_of(at)], out_sem.at[q])
-
-        @pl.when(k > 0)
-        def _():
-            each(0, chunks, lambda q: put_zero(q, k - 1).wait())
+            yl[rows_of(q1), :] = _nn(xa, invp[...])
+            xl[rows_of(q1), :] = xa
+            xl[rows_of(q2), :] = xb
 
         @pl.when(more)
         def _():
-            def solve_left(q):
-                xl[rows_of(q), :] = _nt(left[now, pl.ds(QS * q, QS)].reshape(QS * TR, SB), invp[par])
-
-            each((k + 1) // QS, chunks, solve_left)
-        @pl.when(more)
-        def _():
-            each(w0, jnp.minimum((k + 2) // WS + 1, parts), lambda w: relay_two(now, w))
-            xrt[:, cols_of(pair, 2)] = _nt(invp[par], right[now, pl.ds(pair, 2)].reshape(4 * TR, SB))
+            cs = cols_of(pair, 2)
+            slot = (k + 1) % 3
+
+            def advance(q):
+                qa, qb = jnp.minimum(q + 1, chunks - 1), jnp.minimum(q + 2, chunks - 1)
+                xb = _nt(chunk_of(qb), invp[...])
+                ya = _nn(xl[rows_of(qa), :], invp[...])
+                new = mat[rows_of(q), cs] - _nt(yl[rows_of(q), :], right[now, pl.ds(pair, 2)].reshape(4 * TR, SB))
+                mat[rows_of(q), cs] = new
+                left[slot, pl.ds(QS * q, QS), :, pl.ds(own, TC)] = new[:, :TC].reshape(QS, TR, TC)
+                yl[rows_of(qa), :] = ya
+                xl[rows_of(qb), :] = xb
+
+                @pl.when(k < steps - 2)
+                def _():
+                    for i in range(PER):
+                        @pl.when(PER * q + i >= (k + 2) // WS)
+                        def _():
+                            stage(k + 1, PER * q + i)
+
+                    @pl.when(q == (k + 2) // QS)
+                    def _():
+                        stage_small(k + 1)
+
+            each(q1, chunks, advance)
 
         def clear_above(i):
             xl[pl.ds(pl.multiple_of(TR * i, TR), TR), :] = jnp.zeros((TR, SB), F32)
@@ -386,18 +433,6 @@
         each(0, q0, lambda q: put_zero(q, k).start())
         each(q0, chunks, lambda q: put(q).start())
 
-        @pl.when(more)
-        def _():
-            cs = cols_of(pair, 2)
-
-            def update(q):
-                mat[rows_of(q), cs] = mat[rows_of(q), cs] - _nn(xl[rows_of(q), :], xrt[:, cs])
-
-            each((k + 1) // QS, chunks, update)
-
-        @pl.when(k > 0)
-        def _():
-            each(k // WS, parts, lambda w: sent(last, w))
         return carry
 
     lax.fori_loop(0, steps, step, 0)
@@ -422,21 +457,21 @@
                 vm(3, steps, TR, SB),
                 vm(3, steps, 2, TR, SB),
                 vm(rows, SB),
-                vm(SB, local_cols),
-                vm(2, 8, 2 * TR, TC),
+                vm(rows, SB),
+                vm(3, 8, 2 * TR, TC),
                 vm(SB, SB),
                 vm(LANES, LANES),
                 vm(SB, SB),
                 vm(SB, SB),
-                vm(2, SB, SB),
+                vm(SB, SB),
                 vm(SB, SB),
                 vm(QS * TR, TC),
                 dma((chunks + 1,)),
                 dma((chunks,)),
-                dma((2, 4)),
-                dma((2, 4)),
-                dma((2, 3)),
-                dma((2, 3)),
+                dma((3, 4)),
+                dma((3, 4)),
+                dma((3, 3)),
+                dma((3, 3)),
                 dma((3, parts)),
                 dma((3, parts)),
                 dma((3, parts, 2)),
@@ -444,7 +479,7 @@
                 dma((3, parts, 2)),
                 dma((3, parts, 2)),
             ],
-            compiler_params=pltpu.CompilerParams(has_side_effects=True, vmem_limit_bytes=67043328),
+            compiler_params=pltpu.CompilerParams(collective_id=0, has_side_effects=True, vmem_limit_bytes=67043328),
             name="cholesky",
         )(blocks.reshape(rows, local_cols))
         return out.reshape(row_blocks, block_size, local_cols)

time: 780 us -> 683 us (0.88)
  Pallas kernels: 757 us -> 660 us
    pallas_call x1, Pallas kernels: 757 us -> 660 us  [local_factor(): pl.pallas_call(lambda *refs: _kernel(steps, *refs), out_shape=jax.ShapeDt...]
where the time goes in v3:
time: 683 us
  Pallas kernels  660 us (97%)
  local copies, waits for them, and re-layouts  23 us (3%)
    pallas_call x1, Pallas kernels, local_factor(): pl.pallas_call(lambda *refs: _kernel(steps, *refs), out_shape=jax.ShapeDt...  660 us
    unnamed x1, local copies, waits for them, and re-layouts  23 us

profile of v3, /device:TPU:0, one launch (start us, length us, event | category | flops | bytes accessed | tf_op | source)
XLA Modules:
  0.0 683.1 jit_solution(16143911170351409708)
XLA Ops:
  0.0 660.1 %cholesky.1 = f32[2048,4096]{1,0:T(8,128)} custom-call(f32[2048,4096]{1,0:T(8,128)} %bitcast.3), custom_call_target="tpu_custom_call" | custom-call | tf_op jit(solution)/shard_map/cholesky/pallas_call | solution.py:450
  660.1 23.0 %copy.3 = f32[32,64,4096]{2,1,0:T(8,128)} copy(f32[32,64,4096]{2,1,0:T(8,128)} %bitcast.2) | data formatting | bytes 67108864

commit v4 on v0

v4 whole, which is shorter than its diff:
```python
import jax
import jax.numpy as jnp
from jax import lax
from jax.experimental import pallas as pl
from jax.experimental.pallas import tpu as pltpu
from jax.sharding import PartitionSpec as P

F32 = jnp.float32
FULL = lax.Precision.HIGHEST
SB = 256
TR = 64
TC = 128
LANES = 128
CHUNK = 64
QS = 4
WS = 2
PER = QS // WS
LOT = 6
NARROW = 4
TILE = 512
LAST = 2
ORDER = (0, 2, 1, 3)


def _nn(a, b):
    return lax.dot_general(a, b, (((1,), (0,)), ((), ())), precision=FULL, preferred_element_type=F32)


def _nt(a, b):
    return lax.dot_general(a, b, (((1,), (1,)), ((), ())), precision=FULL, preferred_element_type=F32)


def _swap_middle(x0, x1):
    low = lax.broadcasted_iota(jnp.int32, x0.shape, 1) < LANES // 2
    half = LANES // 2
    return jnp.where(low, x0, pltpu.roll(x1, half, 1)), jnp.where(low, pltpu.roll(x0, half, 1), x1)


def _eliminate(left, right, first, count, group):
    rid = lax.broadcasted_iota(jnp.int32, (group, LANES), 0)
    lid = lax.broadcasted_iota(jnp.int32, (group, LANES), 1)
    upper, inverse = [], []
    for g in range(count // group):
        base = first + group * g
        top_l, top_r = left[:group], right[:group]
        cols = [jnp.broadcast_to(top_l[:, base + j : base + j + 1], (group, LANES)) for j in range(group)]
        scale, row_l, row_r, mult = [], [], [], {}
        for j in range(group):
            inv = lax.rsqrt(cols[j][j : j + 1])
            low = jnp.where(rid > j, cols[j] * inv, 0.0)
            u_l, u_r = top_l[j : j + 1] * inv, top_r[j : j + 1] * inv
            for k in range(j + 1, group):
                mult[j, k] = cols[k][j : j + 1] * inv
                cols[k] = cols[k] - low * mult[j, k]
            top_l = jnp.where(rid == j, u_l, top_l - low * u_l)
            top_r = jnp.where(rid == j, u_r, top_r - low * u_r)
            scale.append(inv)
            row_l.append(u_l)
            row_r.append(u_r)
        upper.append(jnp.where(lid >= rid + base, top_l, 0.0))
        inverse.append(top_r)
        rest = count - group * (g + 1)
        if rest == 0:
            break
        next_l, next_r = [], []
        for start in range(0, rest, CHUNK):
            stop = min(start + CHUNK, rest)
            a, b = left[group + start : group + stop], right[group + start : group + stop]
            below = [jnp.broadcast_to(a[:, base + j : base + j + 1], (stop - start, LANES)) for j in range(group)]
            for j in range(group):
                low = below[j] * scale[j]
                for k in range(j + 1, group):
                    below[k] = below[k] - low * mult[j, k]
                a = a - low * row_l[j]
                b = b - low * row_r[j]
            next_l.append(a)
            next_r.append(b)
        left = jnp.concatenate(next_l, 0) if len(next_l) > 1 else next_l[0]
        right = jnp.concatenate(next_r, 0) if len(next_r) > 1 else next_r[0]
    return upper, inverse


def _factor128(src, group, split):
    lane = lax.broadcasted_iota(jnp.int32, (LANES, LANES), 1)
    rows = lax.broadcasted_iota(jnp.int32, (LANES, LANES), 0)
    left, right = src, jnp.where(lane == rows, 1.0, 0.0).astype(F32)
    upper, inverse = [], []
    for first in range(0, LANES, split):
        u, w = _eliminate(left[:split], right[:split], first, split, group)
        upper += u
        inverse += w
        if first + split < LANES:
            u, w = jnp.concatenate(u, 0), jnp.concatenate(w, 0)
            t = u.T[first + split :]
            left, right = left[split:] - _nn(t, u), right[split:] - _nn(t, w)
    return upper, inverse


def _half(diag, upper, lower, inv, h, group, split):
    span = pl.ds(pl.multiple_of(LANES * h, LANES), LANES)
    u, w = _factor128(diag[span, span], group, split)
    for i in range(LANES // group):
        at = pl.ds(pl.multiple_of(LANES * h + group * i, group), group)
        upper[group * i : group * i + group, :] = u[i]
        inv[at, span] = w[i]
    lower[span, span] = upper[...].T


def _middle(diag, lower, inv):
    l10 = _nt(diag[LANES:, :LANES], inv[:LANES, :LANES])
    lower[LANES:, :LANES] = l10
    diag[LANES:, LANES:] = diag[LANES:, LANES:] - _nt(l10, l10)


def _inverse(lower, inv, invp):
    inv[LANES:, :LANES] = -_nn(inv[LANES:, LANES:], _nn(lower[LANES:, :LANES], inv[:LANES, :LANES]))
    inv[:LANES, LANES:] = jnp.zeros((LANES, LANES), F32)
    lower[:LANES, LANES:] = jnp.zeros((LANES, LANES), F32)
    for i in range(4):
        at = slice(TR * ORDER[i], TR * ORDER[i] + TR)
        s0, s1 = _swap_middle(inv[at, :LANES], inv[at, LANES:])
        invp[TR * i : TR * i + TR, :LANES] = s0
        invp[TR * i : TR * i + TR, LANES:] = s1


def _own_rows(lower, r):
    mine = pl.ds(pl.multiple_of(TR * r, TR), TR)
    return _swap_middle(lower[mine, :LANES], lower[mine, LANES:])


def _each(lo, hi, body):
    def step(i, carry):
        body(i)
        return carry

    lax.fori_loop(lo, hi, step, 0)


def _rows_of(q):
    return pl.ds(pl.multiple_of(QS * TR * q, QS * TR), QS * TR)


def _cols_of(k, n=1):
    return pl.ds(pl.multiple_of(TC * k, TC), n * TC)


def _kernel(steps, a_hbm, out_hbm, rest_hbm, mat, left, right, xl, yl, pieces, diag, upper, lower, inv, invp, a1, pair,
            load_sem, out_sem, sg_send, sg_recv, fw_send, fw_recv, f1_send, f1_recv, f2_send, f2_recv, f3_send, f3_recv):
    r = lax.axis_index("row")
    c = lax.axis_index("col")
    x = r // 2
    p = r % 2
    me = r * 2 + c
    major = p == c
    minor = p != c
    chunks = steps // QS
    parts = steps // WS
    end = steps - LAST
    late = steps - 8
    rows, cols = steps * TR, steps * TC
    tiles = rows // TILE
    wide_u = max(u for u in range(2 * tiles) if sum(tiles - s // 2 for s in range(u, 2 * tiles)) > 4)
    own = pl.multiple_of(c * TC, TC)
    other = pl.multiple_of((1 - c) * TC, TC)
    xi = (r + 2) % 4
    y_peer = {"row": r, "col": 1 - c}
    x_peer = {"row": xi, "col": c}
    z_peer = {"row": xi, "col": 1 - c}
    d_peer = {"row": 2 * x + 1 - p, "col": c}
    peers = (d_peer, y_peer, x_peer, z_peer)
    each, rows_of, cols_of = _each, _rows_of, _cols_of

    def small(slot, i, n):
        ref = pieces.at[slot, me, pl.ds(0, n * TR)]
        return pltpu.make_async_remote_copy(ref, ref, sg_send.at[slot, i], sg_recv.at[slot, i], device_id=peers[i])

    sources = (None, r * 2 + 1 - c, xi * 2 + c, xi * 2 + 1 - c)

    def forward(slot, i, n):
        ref = pieces.at[slot, sources[i], pl.ds(0, n * TR)]
        return pltpu.make_async_remote_copy(ref, ref, fw_send.at[slot, i - 1], fw_recv.at[slot, i - 1], device_id=d_peer)

    def by_size(k, body):
        for n, chosen in ((2, k < late), (3, k >= late)):
            @pl.when(chosen)
            def _():
                body(n)

    def start_small(k):
        def body(n):
            for i in range(4):
                small((k + 3) % 3, i, n).start()

        by_size(k, body)

    def forward_small(k):
        def body(n):
            small((k + 3) % 3, 0, n).wait_recv()
            for i in range(1, 4):
                small((k + 3) % 3, i, n).wait_recv()
                forward((k + 3) % 3, i, n).start()

        by_size(k, body)

    def finish_small(k):
        def body(n):
            for i in range(1, 4):
                forward((k + 3) % 3, i, n).wait_recv()
            for i in range(4):
                small((k + 3) % 3, i, n).wait_send()
            for i in range(1, 4):
                forward((k + 3) % 3, i, n).wait_send()

        by_size(k, body)

    def f1(slot, w):
        ref = left.at[slot, pl.ds(WS * w, WS), :, pl.ds(own, TC)]
        return pltpu.make_async_remote_copy(ref, ref, f1_send.at[slot, w], f1_recv.at[slot, w], device_id=y_peer)

    def f2(slot, w, h, at):
        return pltpu.make_async_remote_copy(left.at[slot, pl.ds(WS * w, WS), :, pl.ds(at, TC)],
                                            right.at[slot, pl.ds(WS * w, WS), x, :, pl.ds(at, TC)],
                                            f2_send.at[slot, w, h], f2_recv.at[slot, w, h], device_id=x_peer)

    def f3a(slot, w):
        return pltpu.make_async_remote_copy(left.at[slot, pl.ds(WS * w, WS)], right.at[slot, pl.ds(WS * w, WS), x],
                                            f3_send.at[slot, w, 0], f3_recv.at[slot, w, 0], device_id=d_peer)

    def f3b(slot, w):
        ref = right.at[slot, pl.ds(WS * w, WS), 1 - x]
        return pltpu.make_async_remote_copy(ref, ref, f3_send.at[slot, w, 1], f3_recv.at[slot, w, 1], device_id=d_peer)

    def relay(k, w):
        slot = k % 3
        f1(slot, w).wait_recv()

        @pl.when(major & (k < end - 1))
        def _():
            f2(slot, w, 1, other).start()
            f3a(slot, w).start()
            right[slot, pl.ds(WS * w, WS), x] = left[slot, pl.ds(WS * w, WS)]

    def arrived(slot, w):
        f2(slot, w, 0, own).wait_recv()
        f2(slot, w, 1, other).wait_recv()

    def take(slot, w):
        f3a(slot, w).wait_recv()
        f3b(slot, w).wait_recv()

    def sent(slot, w):
        f1(slot, w).wait_send()

        @pl.when(major)
        def _():
            f2(slot, w, 0, own).wait_send()
            f2(slot, w, 1, other).wait_send()
            f3a(slot, w).wait_send()

    head = min(3 * TC, cols)

    def load_first():
        return pltpu.make_async_copy(a_hbm.at[:TR, :TC], pieces.at[2, me, TR : 2 * TR], load_sem.at[chunks + 1])

    def load_head():
        return pltpu.make_async_copy(a_hbm.at[:, pl.ds(0, head)], mat.at[:, pl.ds(0, head)], load_sem.at[chunks])

    def load_rest(q):
        wide = min((QS * TC) * (q + 2), cols) - head
        at = (pl.ds(QS * TR * q, QS * TR), pl.ds(head, wide))
        return pltpu.make_async_copy(a_hbm.at[at], mat.at[at], load_sem.at[q])

    load_first().start()
    load_head().start()
    barrier = pltpu.get_barrier_semaphore()
    for peer in peers:
        pl.semaphore_signal(barrier, inc=1, device_id=peer)
    pieces[2, me, :TR] = jnp.zeros((TR, TC), F32)
    pieces[2, me, 2 * TR :] = jnp.zeros((TR, TC), F32)
    load_first().wait()
    pl.semaphore_wait(barrier, len(peers))
    start_small(-1)
    load_head().wait()
    for q in range(chunks):
        load_rest(q).start()

    def place_diag(slot):
        for i in range(4):
            s0, s1 = _swap_middle(pieces[slot, 2 * i, TR : 2 * TR, :], pieces[slot, 2 * i + 1, TR : 2 * TR, :])
            diag[TR * i : TR * i + TR, :LANES] = s0
            diag[TR * i : TR * i + TR, LANES:] = s1

    def place_next(slot):
        for i in range(4):
            a1[TR * i : TR * i + TR, :LANES] = pieces[slot, 2 * i, :TR, :]
            a1[TR * i : TR * i + TR, LANES:] = pieces[slot, 2 * i + 1, :TR, :]

    def stage(k, w):
        f1(k % 3, w).start()

    def stage_x(k, lot):
        @pl.when(major & (k < end - 1))
        def _():
            w0 = (k + 1) // WS
            cut = jnp.minimum(w0 + LOT, parts)
            each(jnp.where(lot == 0, w0, cut), jnp.where(lot == 0, cut, parts), lambda w: f2(k % 3, w, 0, own).start())

    def stage_small(k):
        slot = k % 3
        one = pl.ds(pl.multiple_of(TR * (k + 1), TR), TR)
        two = pl.ds(pl.multiple_of(TR * jnp.minimum(k + 2, steps - 1), TR), TR)
        pieces[slot, me, :TR, :] = mat[one, cols_of(k)]
        pieces[slot, me, TR : 2 * TR, :] = mat[one, cols_of(k + 1)]
        pieces[slot, me, 2 * TR :, :] = mat[two, cols_of(k)]
        start_small(k)

    def first(q):
        left[0, pl.ds(QS * q, QS), :, pl.ds(own, TC)] = mat[rows_of(q), :TC].reshape(QS, TR, TC)

    each(0, chunks, first)
    stage(0, 0)
    stage(0, 1)
    stage_small(0)
    each(2, parts, lambda w: stage(0, w))
    stage_x(0, 0)
    forward_small(-1)
    finish_small(-1)
    place_diag(2)

    def step(k, carry):
        now = k % 3
        last = (k + 2) % 3
        q0 = k // QS
        w0 = (k + 1) // WS
        w1 = jnp.minimum((k + 2) // WS, parts - 1)

        u0 = (k + 2) // QS
        count = 0
        for u in range(2 * tiles):
            count = count + jnp.where(u >= u0, tiles - u // 2, 0)
        count = jnp.where(k > 0, count, 0)

        inner = 0
        for u in range(2 * tiles):
            inner = inner + jnp.where((u >= u0) & (u < u0 + 3), tiles - u // 2, 0)
        inner = jnp.minimum(inner, 8)

        def tile(i, among=count):
            u, past_of, total = 0, 0, 0
            for s in range(2 * tiles):
                total = total + jnp.where(s >= u0, tiles - s // 2, 0)
                past = i >= total
                u = u + jnp.where(past, 1, 0)
                past_of = jnp.where(past, total, past_of)
            live = i < among
            t = jnp.where(live, u // 2 + i - past_of, 0)
            seen = jnp.where(live, u, u0)
            u = jnp.where(live, u, 2 * tiles - 1)
            rs = pl.ds(pl.multiple_of(TILE * t, TILE), TILE)
            cs = pl.ds(pl.multiple_of(TILE * u, TILE), TILE)
            mat[rs, cs] = mat[rs, cs] - _nt(yl[rs, :], right[last, pl.ds(QS * seen, QS)].reshape(TILE, SB))

        lo = k // WS
        mid = jnp.minimum((k + 1) // WS + 1, parts)
        s1 = jnp.clip(PER * (u0 + 2), mid, parts)
        s2 = jnp.clip(PER * (u0 + 3), mid, parts)

        def pass_on(slot, a, b):
            def body(w):
                arrived(slot, w)
                f3b(slot, w).start()

            each(a, b, body)

        def finish_exchange(passed, taken):
            @pl.when((k > 0) & major)
            def _():
                pass_on(last, *passed)

            @pl.when((k > 0) & minor)
            def _():
                each(*taken, lambda w: take(last, w))

        def finish_pair(side):
            zero = jnp.zeros((2, 2, TR, SB), F32)

            @pl.when((k > 0) & side)
            def _():
                @pl.when((k <= late) & major)
                def _():
                    each(lo, mid, lambda w: f3b(last, w).wait_send())

                @pl.when((k > late) & major)
                def _():
                    each(lo, mid, lambda w: arrived(last, w))

                @pl.when((k > late) & minor)
                def _():
                    each(lo, mid, lambda w: take(last, w))

                right[last, pl.ds(k, 2)] = zero

                @pl.when((k > late) & major)
                def _():
                    each(lo, mid, lambda w: f3b(last, w).start())

        def relay_pair():
            @pl.when(k < late)
            def _():
                each(w0, w1 + 1, lambda w: relay(k, w))

            stage_x(k, 1)

        wide = (k > 0) & (u0 <= wide_u)

        @pl.when(wide)
        def _():
            finish_pair(True)
            finish_exchange((s1, s2), (mid, s1))

            @pl.when(k == 1)
            def _():
                for q in range(chunks):
                    load_rest(q).wait()

            def half(h):
                @pl.when(h == 1)
                def _():
                    _middle(diag, lower, inv)
                    finish_exchange((s2, parts), (s1, s2))

                for i in range(4):
                    tile(4 * h + i, inner)
                _half(diag, upper, lower, inv, h, 8, LANES)

                @pl.when(h == 0)
                def _():
                    relay_pair()

            each(0, 2, half)

        @pl.when(jnp.logical_not(wide))
        def _():
            finish_pair(major)
            finish_exchange((mid, parts), (mid, mid))
            _half(diag, upper, lower, inv, 0, 16, LANES // 2)
            relay_pair()
            finish_pair(minor)
            finish_exchange((mid, mid), (mid, parts))
            _middle(diag, lower, inv)

        @pl.when(jnp.logical_not(wide))
        def _():
            for i in range(NARROW):
                tile(i)
            _half(diag, upper, lower, inv, 1, 8, LANES)

        forward_small(k)

        @pl.when((k < late) & major)
        def _():
            def body(w):
                arrived(now, w)
                f3b(now, w).start()

            each(w0, w1 + 1, body)

        _inverse(lower, inv, invp)

        @pl.when(wide)
        def _():
            finish_exchange((mid, mid), (s2, parts))

        def put(q, at):
            return pltpu.make_async_copy(xl.at[rows_of(q), pl.ds(own, TC)], out_hbm.at[rows_of(q), cols_of(at)], out_sem.at[q])

        q1 = (k + 1) // QS
        q2 = jnp.minimum(q1 + 1, chunks - 1)
        inner = jnp.where(wide, inner, jnp.minimum(count, NARROW))
        over = count - inner
        upto = jnp.minimum(jnp.maximum(w0 + 7 + (7 * over) // 10, PER * (q2 + 1)), parts)
        since = jnp.where(k < late, w1 + 1, w0)
        many = jnp.maximum(upto - since, 1)

        def share(j):
            return inner + (over * j) // many

        def between(j):
            each(share(j), share(j + 1), tile)

            @pl.when(since + j < upto)
            def _():
                relay(k, since + j)

        each(0, many, between)

        @pl.when(k > 0)
        def _():
            each(k // WS, parts, lambda w: sent(last, w))

            @pl.when(major)
            def _():
                each(jnp.where(k <= late, mid, lo), parts, lambda w: f3b(last, w).wait_send())

            each((k - 1) // QS, chunks, lambda q: put(q, k - 1).wait())

        def chunk_of(q):
            return left[now, pl.ds(QS * q, QS)].reshape(QS * TR, SB)

        def pair_of_pieces():
            for s in range(2):
                for h in range(2):
                    own_class = pieces.at[now, 2 * (c + 2 * s) + h]
                    pair[TR * s : TR * s + TR, TC * h : TC * h + TC] = own_class[:TR, :]
                    pair[TR * (2 + s) : TR * (2 + s) + TR, TC * h : TC * h + TC] = own_class[2 * TR :, :]

        finish_small(k)
        place_next(now)
        place_diag(now)

        @pl.when(k < late)
        def _():
            @pl.when(minor)
            def _():
                each(w0, w1 + 1, lambda w: take(now, w))

            pair[...] = right[now, pl.ds(k + 1, 2)].reshape(4 * TR, SB)

        @pl.when(k >= late)
        def _():
            pair_of_pieces()

        x1 = _nt(a1[...], invp[...])
        xa = _nt(chunk_of(q1), invp[...])
        xb = _nt(chunk_of(q2), invp[...])
        diag[...] = diag[...] - _nt(x1, x1)
        yl[rows_of(q1), :] = _nn(xa, invp[...])
        xl[rows_of(q1), :] = xa
        xl[rows_of(q2), :] = xb

        cs = cols_of(k + 1, 2)
        slot = (k + 1) % 3

        def advance(q):
            qa, qb = jnp.minimum(q + 1, chunks - 1), jnp.minimum(q + 2, chunks - 1)
            each(jnp.maximum(upto, PER * (q + 2)), jnp.minimum(PER * (q + 3), parts), lambda w: relay(k, w))
            xb = _nt(chunk_of(qb), invp[...])
            ya = _nn(xl[rows_of(qa), :], invp[...])
            new = mat[rows_of(q), cs] - _nt(yl[rows_of(q), :], pair[...])
            mat[rows_of(q), cs] = new
            left[slot, pl.ds(QS * q, QS), :, pl.ds(own, TC)] = new[:, :TC].reshape(QS, TR, TC)
            yl[rows_of(qa), :] = ya
            xl[rows_of(qb), :] = xb

            for i in range(PER):
                @pl.when((k < end - 1) & (PER * q + i >= (k + 2) // WS))
                def _():
                    stage(k + 1, PER * q + i)

            @pl.when(q == jnp.minimum(k + 3, steps - 1) // QS)
            def _():
                stage_small(k + 1)

        each(q1, chunks, advance)
        stage_x(k + 1, 0)

        def clear_above(i):
            xl[pl.ds(pl.multiple_of(TR * i, TR), TR), :] = jnp.zeros((TR, SB), F32)

        each(QS * q0, k, clear_above)
        at = pl.ds(pl.multiple_of(TR * k, TR), TR)
        xl[at, :LANES], xl[at, LANES:] = _own_rows(lower, r)
        each(q0, chunks, lambda q: put(q, k).start())

        u1 = (k + 3) // QS
        next_mid = jnp.minimum((k + 2) // WS + 1, parts)

        @pl.when(major & (u1 <= wide_u))
        def _():
            pass_on(now, next_mid, jnp.clip(PER * (u1 + 2), next_mid, parts))
        return carry

    lax.fori_loop(0, end, step, 0)

    def leave(src, i):
        return pltpu.make_async_copy(src, rest_hbm.at[i], load_sem.at[i])

    slot = end % 3
    leave(diag, 0).start()
    forward_small(end)
    finish_small(end)
    place_next(slot)
    leave(a1, 1).start()
    for i in range(4):
        s0, s1 = _swap_middle(pieces[slot, 2 * i, TR : 2 * TR, :], pieces[slot, 2 * i + 1, TR : 2 * TR, :])
        pair[TR * i : TR * i + TR, :LANES] = s0
        pair[TR * i : TR * i + TR, LANES:] = s1
    leave(pair, 2).start()
    for i, src in enumerate((diag, a1, pair)):
        leave(src, i).wait()
    each((end - 1 + 1) // WS, parts, lambda w: f1((end - 1) % 3, w).wait_send())

    def drain(q):
        pltpu.make_async_copy(xl.at[rows_of(q), pl.ds(own, TC)], out_hbm.at[rows_of(q), cols_of(end - 1)], out_sem.at[q]).wait()

    each((end - 1) // QS, chunks, drain)


def _finish(steps, part_hbm, rest, out_hbm, buf, zeros, diag, upper, lower, inv, invp, in_sem, out_sem, zero_sem):
    r = lax.axis_index("row")
    c = lax.axis_index("col")
    chunks = steps // QS
    rows, cols = steps * TR, steps * TC
    kept = cols - LAST * TC
    own = pl.multiple_of(c * TC, TC)

    def block(q):
        return (pl.ds(QS * TR * q, QS * TR), pl.ds(0, min(QS * TC * (q + 1), kept)))

    def load(q):
        return pltpu.make_async_copy(part_hbm.at[block(q)], buf.at[block(q)], in_sem.at[q])

    def store(q):
        return pltpu.make_async_copy(buf.at[block(q)], out_hbm.at[block(q)], out_sem.at[q])

    def blank(q):
        wide = cols - QS * TC * (q + 1)
        return pltpu.make_async_copy(zeros.at[:, pl.ds(0, wide)],
                                     out_hbm.at[pl.ds(QS * TR * q, QS * TR), pl.ds(QS * TC * (q + 1), wide)], zero_sem.at[q])

    tail = (pl.ds(rows - QS * TR, QS * TR), pl.ds(kept, LAST * TC))
    final = pltpu.make_async_copy(buf.at[tail], out_hbm.at[tail], zero_sem.at[chunks - 1])

    for q in range(chunks):
        load(q).start()
    zeros[...] = jnp.zeros_like(zeros)
    buf[tail] = jnp.zeros((QS * TR, LAST * TC), F32)

    def own_half(s0, s1):
        return jnp.where(c == 0, s0, s1)

    diag[...] = rest[0]
    for k in range(LAST):
        last_rows = slice(rows - (LAST - k) * TR, rows - (LAST - k - 1) * TR)
        at = slice(kept + k * TC, kept + k * TC + TC)
        _half(diag, upper, lower, inv, 0, 16, LANES // 2)
        _middle(diag, lower, inv)
        _half(diag, upper, lower, inv, 1, 16, LANES // 2)
        if k == 0:
            for q in range(chunks):
                load(q).wait()
                store(q).start()
            for q in range(chunks - 1):
                blank(q).start()
        if k < LAST - 1:
            _inverse(lower, inv, invp)
            x1 = _nt(rest[1], invp[...])
            diag[...] = rest[2] - _nt(x1, x1)
            upper_x = inv
            upper_x[...] = x1
            mine = pl.ds(pl.multiple_of(TR * r, TR), TR)
            buf[rows - TR :, at] = upper_x[mine, pl.ds(own, TC)]
        else:
            lower[:LANES, LANES:] = jnp.zeros((LANES, LANES), F32)
        buf[last_rows, at] = own_half(*_own_rows(lower, r))
    final.start()
    for q in range(chunks):
        store(q).wait()
    for q in range(chunks - 1):
        blank(q).wait()
    final.wait()


def solution(mesh):
    def local_factor(blocks):
        row_blocks, block_size, local_cols = blocks.shape
        rows = row_blocks * block_size
        steps = local_cols // TC
        chunks, parts = steps // QS, steps // WS
        dma = pltpu.SemaphoreType.DMA
        vm = lambda *s: pltpu.VMEM(s, F32)
        anywhere = pl.BlockSpec(memory_space=pl.ANY)
        shape = jax.ShapeDtypeStruct((rows, local_cols), F32)
        part, rest = pl.pallas_call(
            lambda *refs: _kernel(steps, *refs),
            out_shape=(shape, jax.ShapeDtypeStruct((3, SB, SB), F32)),
            in_specs=[anywhere],
            out_specs=(anywhere, anywhere),
            scratch_shapes=[
                vm(rows, local_cols),
                vm(3, steps, TR, SB),
                vm(3, steps, 2, TR, SB),
                vm(rows, SB),
                vm(rows, SB),
                vm(3, 8, 3 * TR, TC),
                vm(SB, SB),
                vm(LANES, LANES),
                vm(SB, SB),
                vm(SB, SB),
                vm(SB, SB),
                vm(SB, SB),
                vm(SB, SB),
                dma((chunks + 2,)),
                dma((chunks,)),
                dma((3, 4)),
                dma((3, 4)),
                dma((3, 3)),
                dma((3, 3)),
                dma((3, parts)),
                dma((3, parts)),
                dma((3, parts, 2)),
                dma((3, parts, 2)),
                dma((3, parts, 2)),
                dma((3, parts, 2)),
            ],
            compiler_params=pltpu.CompilerParams(collective_id=0, has_side_effects=True, vmem_limit_bytes=67043328),
            name="factor",
        )(blocks.reshape(rows, local_cols))
        out = pl.pallas_call(
            lambda *refs: _finish(steps, *refs),
            out_shape=shape,
            in_specs=[anywhere, pl.BlockSpec(memory_space=pltpu.VMEM)],
            out_specs=anywhere,
            scratch_shapes=[
                vm(rows, local_cols),
                vm(QS * TR, local_cols - QS * TC),
                vm(SB, SB),
                vm(LANES, LANES),
                vm(SB, SB),
                vm(SB, SB),
                vm(SB, SB),
                dma((chunks,)),
                dma((chunks,)),
                dma((chunks,)),
            ],
            compiler_params=pltpu.CompilerParams(vmem_limit_bytes=60 * 2**20),
            name="finish",
        )(part, rest)
        return out.reshape(row_blocks, block_size, local_cols)

    spec = P(("part", "row"), None, "col")
    return jax.shard_map(local_factor, mesh=mesh, in_specs=(spec,), out_specs=spec, check_vma=False)
```

time: 14000 us -> 632 us (0.05)
  waiting for transfers between devices: 4610 us -> 0 us
  matrix products: 3470 us -> 0 us
  blocking collectives: 2410 us -> 0 us
  other arithmetic: 2280 us -> 0 us
  local copies, waits for them, and re-layouts: 1170 us -> 0 us
  Pallas kernels: 0 us -> 632 us
    dot_general x127 -> x0, matrix products: 3410 us -> none  [local_factor(): lax.dot_general(row_panel.reshape(trail_rows * block_size, block_size), c...]
    psum x115 -> x0, waiting for transfers between devices: 2900 us -> none  [local_factor(): lax.psum(jnp.where(keep_rows & on_col, solved.reshape(trail_rows, block_s...]
    all_gather x67 -> x0, waiting for transfers between devices: 1710 us -> none  [local_factor(): lax.all_gather(row_panel, 'row', axis=1)]
    another operation x642 -> x0, other arithmetic: 1560 us -> none  [the longest x384 846 us: local_factor(): diag_fac = jnp.linalg.cholesky(diag_sum)]
    psum x140 -> x0, blocking collectives: 1460 us -> none  [the longest x128 1350 us: local_factor(): diag_sum = lax.psum(jnp.where(on_row, diag_local, 0.0), 'row')]
    all_gather x60 -> x0, blocking collectives: 957 us -> none  [local_factor(): lax.all_gather(row_panel, 'row', axis=1)]
    pallas_call x0 -> x2, Pallas kernels: none -> 632 us  [the longest x1 613 us: local_factor(): pl.pallas_call(lambda *refs: _kernel(steps, *refs), out_shape=(shape, jax...]
    scatter x253 -> x0, other arithmetic: 495 us -> none  [the longest x127 267 us: local_factor(): blocks.at[row_lo:, :, diag_lo:diag_hi]]
  transfers between devices with their start and end apart: 182 -> 0, of which waited for: 182 -> 0; matrix products, arithmetic and copies ran while one was open for 1% -> 0% of each run, Pallas kernels for 0% -> 0%
where the time goes in v4:
time: 632 us
  Pallas kernels  632 us (100%)
    pallas_call x1, Pallas kernels, local_factor(): pl.pallas_call(lambda *refs: _kernel(steps, *refs), out_shape=(shape, jax...  613 us
    pallas_call x1, Pallas kernels, local_factor(): pl.pallas_call(lambda *refs: _finish(steps, *refs), out_shape=shape, in_s...  18.8 us

profile of v4, /device:TPU:0, one launch (start us, length us, event | category | flops | bytes accessed | tf_op | source)
XLA Modules:
  0.0 632.1 jit_solution(1309018109112702498)
XLA Ops:
  0.0 613.2 %factor.1 = (f32[2048,4096]{1,0:T(8,128)}, f32[3,256,256]{2,1,0:T(8,128)}) custom-call(f32[2048,4096]{1,0:T(8,128)} %bitcast.2), custom_call_target="tpu_custom_call" | custom-call | tf_op jit(solution)/shard_map/factor/pallas_call | solution.py:684
  613.2 18.8 %finish.1 = f32[2048,4096]{1,0:T(8,128)} custom-call(f32[2048,4096]{1,0:T(8,128)} %get-tuple-element.7.refs_0_, f32[3,256,256]{2,1,0:T(8,128)} %get-tuple-element.8.refs_1_), custom_call_target="tpu_custom_call" | custom-call | tf_op jit(solution)/shard_map/finish/pallas_call | solution.py:719

commit v5 on v4

--- a/solution.py
+++ b/solution.py
@@ -11,7 +11,7 @@
 TR = 64
 TC = 128
 LANES = 128
-CHUNK = 64
+CHUNK = 32
 QS = 4
 WS = 2
 PER = QS // WS
@@ -39,6 +39,8 @@
 def _eliminate(left, right, first, count, group):
     rid = lax.broadcasted_iota(jnp.int32, (group, LANES), 0)
     lid = lax.broadcasted_iota(jnp.int32, (group, LANES), 1)
+    here, under = [rid == j for j in range(group)], [rid > j for j in range(group)]
+    diff = lid - rid
     upper, inverse = [], []
     for g in range(count // group):
         base = first + group * g
@@ -47,17 +49,17 @@
         scale, row_l, row_r, mult = [], [], [], {}
         for j in range(group):
             inv = lax.rsqrt(cols[j][j : j + 1])
-            low = jnp.where(rid > j, cols[j] * inv, 0.0)
+            low = jnp.where(under[j], cols[j] * inv, 0.0)
             u_l, u_r = top_l[j : j + 1] * inv, top_r[j : j + 1] * inv
             for k in range(j + 1, group):
                 mult[j, k] = cols[k][j : j + 1] * inv
                 cols[k] = cols[k] - low * mult[j, k]
-            top_l = jnp.where(rid == j, u_l, top_l - low * u_l)
-            top_r = jnp.where(rid == j, u_r, top_r - low * u_r)
+            top_l = jnp.where(here[j], u_l, top_l - low * u_l)
+            top_r = jnp.where(here[j], u_r, top_r - low * u_r)
             scale.append(inv)
             row_l.append(u_l)
             row_r.append(u_r)
-        upper.append(jnp.where(lid >= rid + base, top_l, 0.0))
+        upper.append(jnp.where(diff >= base, top_l, 0.0))
         inverse.append(top_r)
         rest = count - group * (g + 1)
         if rest == 0:
@@ -109,11 +111,12 @@
 def _middle(diag, lower, inv):
     l10 = _nt(diag[LANES:, :LANES], inv[:LANES, :LANES])
     lower[LANES:, :LANES] = l10
+    inv[LANES:, :LANES] = _nn(l10, inv[:LANES, :LANES])
     diag[LANES:, LANES:] = diag[LANES:, LANES:] - _nt(l10, l10)
 
 
 def _inverse(lower, inv, invp):
-    inv[LANES:, :LANES] = -_nn(inv[LANES:, LANES:], _nn(lower[LANES:, :LANES], inv[:LANES, :LANES]))
+    inv[LANES:, :LANES] = -_nn(inv[LANES:, LANES:], inv[LANES:, :LANES])
     inv[:LANES, LANES:] = jnp.zeros((LANES, LANES), F32)
     lower[:LANES, LANES:] = jnp.zeros((LANES, LANES), F32)
     for i in range(4):
@@ -145,7 +148,7 @@
 
 
 def _kernel(steps, a_hbm, out_hbm, rest_hbm, mat, left, right, xl, yl, pieces, diag, upper, lower, inv, invp, a1, pair,
-            load_sem, out_sem, sg_send, sg_recv, fw_send, fw_recv, f1_send, f1_recv, f2_send, f2_recv, f3_send, f3_recv):
+            load_sem, out_sem, sg_send, sg_recv, fw_send, fw_recv, f1_send, f1_recv, x_send, f2_recv, f3_send, f3_recv):
     r = lax.axis_index("row")
     c = lax.axis_index("col")
     x = r // 2
@@ -217,18 +220,26 @@
         ref = left.at[slot, pl.ds(WS * w, WS), :, pl.ds(own, TC)]
         return pltpu.make_async_remote_copy(ref, ref, f1_send.at[slot, w], f1_recv.at[slot, w], device_id=y_peer)
 
-    def f2(slot, w, h, at):
+    def f2(slot, w, at):
         return pltpu.make_async_remote_copy(left.at[slot, pl.ds(WS * w, WS), :, pl.ds(at, TC)],
                                             right.at[slot, pl.ds(WS * w, WS), x, :, pl.ds(at, TC)],
-                                            f2_send.at[slot, w, h], f2_recv.at[slot, w, h], device_id=x_peer)
+                                            x_send.at[slot, w], f2_recv.at[slot, w], device_id=x_peer)
 
     def f3a(slot, w):
         return pltpu.make_async_remote_copy(left.at[slot, pl.ds(WS * w, WS)], right.at[slot, pl.ds(WS * w, WS), x],
-                                            f3_send.at[slot, w, 0], f3_recv.at[slot, w, 0], device_id=d_peer)
+                                            x_send.at[slot, w], f3_recv.at[slot, w], device_id=d_peer)
 
     def f3b(slot, w):
         ref = right.at[slot, pl.ds(WS * w, WS), 1 - x]
-        return pltpu.make_async_remote_copy(ref, ref, f3_send.at[slot, w, 1], f3_recv.at[slot, w, 1], device_id=d_peer)
+        return pltpu.make_async_remote_copy(ref, ref, f3_send.at[slot, w], f3_recv.at[slot, w], device_id=d_peer)
+
+    def both_halves(slot, w):
+        ref = right.at[slot, pl.ds(WS * w, WS), 1 - x]
+        return pltpu.make_async_remote_copy(ref, ref, x_send.at[slot, w], f2_recv.at[slot, w], device_id=x_peer)
+
+    def both_classes(slot, w):
+        ref = right.at[slot, pl.ds(WS * w, WS)]
+        return pltpu.make_async_remote_copy(ref, ref, x_send.at[slot, w], f3_recv.at[slot, w], device_id=d_peer)
 
     def relay(k, w):
         slot = k % 3
@@ -236,26 +247,22 @@
 
         @pl.when(major & (k < end - 1))
         def _():
-            f2(slot, w, 1, other).start()
+            f2(slot, w, other).start()
             f3a(slot, w).start()
             right[slot, pl.ds(WS * w, WS), x] = left[slot, pl.ds(WS * w, WS)]
 
     def arrived(slot, w):
-        f2(slot, w, 0, own).wait_recv()
-        f2(slot, w, 1, other).wait_recv()
+        both_halves(slot, w).wait_recv()
 
     def take(slot, w):
-        f3a(slot, w).wait_recv()
-        f3b(slot, w).wait_recv()
+        both_classes(slot, w).wait_recv()
 
     def sent(slot, w):
         f1(slot, w).wait_send()
 
         @pl.when(major)
         def _():
-            f2(slot, w, 0, own).wait_send()
-            f2(slot, w, 1, other).wait_send()
-            f3a(slot, w).wait_send()
+            both_classes(slot, w).wait_send()
 
     head = min(3 * TC, cols)
 
@@ -303,7 +310,7 @@
         def _():
             w0 = (k + 1) // WS
             cut = jnp.minimum(w0 + LOT, parts)
-            each(jnp.where(lot == 0, w0, cut), jnp.where(lot == 0, cut, parts), lambda w: f2(k % 3, w, 0, own).start())
+            each(jnp.where(lot == 0, w0, cut), jnp.where(lot == 0, cut, parts), lambda w: f2(k % 3, w, own).start())
 
     def stage_small(k):
         slot = k % 3
@@ -478,7 +485,9 @@
         q2 = jnp.minimum(q1 + 1, chunks - 1)
         inner = jnp.where(wide, inner, jnp.minimum(count, NARROW))
         over = count - inner
-        upto = jnp.minimum(jnp.maximum(w0 + 7 + (7 * over) // 10, PER * (q2 + 1)), parts)
+        extra = wide & (over > 0)
+        over = jnp.where(extra, over - 1, over)
+        upto = jnp.minimum(jnp.maximum(w0 + 5 + over // 2, PER * (q2 + 1)), parts)
         since = jnp.where(k < late, w1 + 1, w0)
         many = jnp.maximum(upto - since, 1)
 
@@ -530,13 +539,23 @@
         def _():
             pair_of_pieces()
 
-        x1 = _nt(a1[...], invp[...])
-        xa = _nt(chunk_of(q1), invp[...])
-        xb = _nt(chunk_of(q2), invp[...])
-        diag[...] = diag[...] - _nt(x1, x1)
-        yl[rows_of(q1), :] = _nn(xa, invp[...])
-        xl[rows_of(q1), :] = xa
-        xl[rows_of(q2), :] = xb
+        def begin():
+            x1 = _nt(a1[...], invp[...])
+            xa = _nt(chunk_of(q1), invp[...])
+            xb = _nt(chunk_of(q2), invp[...])
+            diag[...] = diag[...] - _nt(x1, x1)
+            yl[rows_of(q1), :] = _nn(xa, invp[...])
+            xl[rows_of(q1), :] = xa
+            xl[rows_of(q2), :] = xb
+
+        @pl.when(extra)
+        def _():
+            tile(count - 1)
+            begin()
+
+        @pl.when(jnp.logical_not(extra))
+        def _():
+            begin()
 
         cs = cols_of(k + 1, 2)
         slot = (k + 1) % 3
@@ -640,29 +659,40 @@
         return jnp.where(c == 0, s0, s1)
 
     diag[...] = rest[0]
-    for k in range(LAST):
-        last_rows = slice(rows - (LAST - k) * TR, rows - (LAST - k - 1) * TR)
-        at = slice(kept + k * TC, kept + k * TC + TC)
-        _half(diag, upper, lower, inv, 0, 16, LANES // 2)
-        _middle(diag, lower, inv)
-        _half(diag, upper, lower, inv, 1, 16, LANES // 2)
-        if k == 0:
+
+    def rows_of_l(k):
+        buf[rows - (LAST - k) * TR : rows - (LAST - k - 1) * TR, kept + k * TC : kept + k * TC + TC] = own_half(*_own_rows(lower, r))
+
+    def half(i):
+        h = i % 2
+
+        @pl.when(h == 1)
+        def _():
+            _middle(diag, lower, inv)
+
+        _half(diag, upper, lower, inv, h, 16, LANES // 2)
+
+        @pl.when(i == 1)
+        def _():
             for q in range(chunks):
                 load(q).wait()
                 store(q).start()
             for q in range(chunks - 1):
                 blank(q).start()
-        if k < LAST - 1:
             _inverse(lower, inv, invp)
             x1 = _nt(rest[1], invp[...])
             diag[...] = rest[2] - _nt(x1, x1)
-            upper_x = inv
-            upper_x[...] = x1
+            rows_of_l(0)
+            invp[...] = x1
             mine = pl.ds(pl.multiple_of(TR * r, TR), TR)
-            buf[rows - TR :, at] = upper_x[mine, pl.ds(own, TC)]
-        else:
+            buf[rows - TR :, kept : kept + TC] = invp[mine, pl.ds(own, TC)]
+
+        @pl.when(i == 3)
+        def _():
             lower[:LANES, LANES:] = jnp.zeros((LANES, LANES), F32)
-        buf[last_rows, at] = own_half(*_own_rows(lower, r))
+            rows_of_l(1)
+
+    _each(0, 2 * LAST, half)
     final.start()
     for q in range(chunks):
         store(q).wait()
@@ -708,10 +738,10 @@
                 dma((3, 3)),
                 dma((3, parts)),
                 dma((3, parts)),
-                dma((3, parts, 2)),
-                dma((3, parts, 2)),
-                dma((3, parts, 2)),
-                dma((3, parts, 2)),
+                dma((3, parts)),
+                dma((3, parts)),
+                dma((3, parts)),
+                dma((3, parts)),
             ],
             compiler_params=pltpu.CompilerParams(collective_id=0, has_side_effects=True, vmem_limit_bytes=67043328),
             name="factor",

time: 632 us -> 626 us (level)
  Pallas kernels: 632 us -> 625 us
    pallas_call x1, Pallas kernels: 613 us -> 606 us  [local_factor(): pl.pallas_call(lambda *refs: _kernel(steps, *refs), out_shape=(shape, jax...]
where the time goes in v5:
time: 626 us
  Pallas kernels  625 us (100%)
    pallas_call x1, Pallas kernels, local_factor(): pl.pallas_call(lambda *refs: _kernel(steps, *refs), out_shape=(shape, jax...  606 us
    pallas_call x1, Pallas kernels, local_factor(): pl.pallas_call(lambda *refs: _finish(steps, *refs), out_shape=shape, in_s...  19.2 us

profile of v5, /device:TPU:0, one launch (start us, length us, event | category | flops | bytes accessed | tf_op | source)
XLA Modules:
  0.0 625.5 jit_solution(2136231159192220155)
XLA Ops:
  0.0 606.2 %factor.1 = (f32[2048,4096]{1,0:T(8,128)}, f32[3,256,256]{2,1,0:T(8,128)}) custom-call(f32[2048,4096]{1,0:T(8,128)} %bitcast.2), custom_call_target="tpu_custom_call" | custom-call | tf_op jit(solution)/shard_map/factor/pallas_call | solution.py:714
  606.2 19.2 %finish.1 = f32[2048,4096]{1,0:T(8,128)} custom-call(f32[2048,4096]{1,0:T(8,128)} %get-tuple-element.7.refs_0_, f32[3,256,256]{2,1,0:T(8,128)} %get-tuple-element.8.refs_1_), custom_call_target="tpu_custom_call" | custom-call | tf_op jit(solution)/shard_map/finish/pallas_call | solution.py:749

commit v6 on v5

--- a/solution.py
+++ b/solution.py
@@ -184,7 +184,10 @@
         return pltpu.make_async_remote_copy(ref, ref, fw_send.at[slot, i - 1], fw_recv.at[slot, i - 1], device_id=d_peer)
 
     def by_size(k, body):
-        for n, chosen in ((2, k < late), (3, k >= late)):
+        if isinstance(k, int) and k < 0:
+            body(1)
+            return
+        for n, chosen in ((2, (k < late) | (k == end)), (3, (k >= late) & (k != end))):
             @pl.when(chosen)
             def _():
                 body(n)
@@ -267,7 +270,7 @@
     head = min(3 * TC, cols)
 
     def load_first():
-        return pltpu.make_async_copy(a_hbm.at[:TR, :TC], pieces.at[2, me, TR : 2 * TR], load_sem.at[chunks + 1])
+        return pltpu.make_async_copy(a_hbm.at[:TR, :TC], pieces.at[2, me, :TR], load_sem.at[chunks + 1])
 
     def load_head():
         return pltpu.make_async_copy(a_hbm.at[:, pl.ds(0, head)], mat.at[:, pl.ds(0, head)], load_sem.at[chunks])
@@ -282,8 +285,6 @@
     barrier = pltpu.get_barrier_semaphore()
     for peer in peers:
         pl.semaphore_signal(barrier, inc=1, device_id=peer)
-    pieces[2, me, :TR] = jnp.zeros((TR, TC), F32)
-    pieces[2, me, 2 * TR :] = jnp.zeros((TR, TC), F32)
     load_first().wait()
     pl.semaphore_wait(barrier, len(peers))
     start_small(-1)
@@ -293,14 +294,14 @@
 
     def place_diag(slot):
         for i in range(4):
-            s0, s1 = _swap_middle(pieces[slot, 2 * i, TR : 2 * TR, :], pieces[slot, 2 * i + 1, TR : 2 * TR, :])
+            s0, s1 = _swap_middle(pieces[slot, 2 * i, :TR, :], pieces[slot, 2 * i + 1, :TR, :])
             diag[TR * i : TR * i + TR, :LANES] = s0
             diag[TR * i : TR * i + TR, LANES:] = s1
 
     def place_next(slot):
         for i in range(4):
-            a1[TR * i : TR * i + TR, :LANES] = pieces[slot, 2 * i, :TR, :]
-            a1[TR * i : TR * i + TR, LANES:] = pieces[slot, 2 * i + 1, :TR, :]
+            a1[TR * i : TR * i + TR, :LANES] = pieces[slot, 2 * i, TR : 2 * TR, :]
+            a1[TR * i : TR * i + TR, LANES:] = pieces[slot, 2 * i + 1, TR : 2 * TR, :]
 
     def stage(k, w):
         f1(k % 3, w).start()
@@ -316,8 +317,8 @@
         slot = k % 3
         one = pl.ds(pl.multiple_of(TR * (k + 1), TR), TR)
         two = pl.ds(pl.multiple_of(TR * jnp.minimum(k + 2, steps - 1), TR), TR)
-        pieces[slot, me, :TR, :] = mat[one, cols_of(k)]
-        pieces[slot, me, TR : 2 * TR, :] = mat[one, cols_of(k + 1)]
+        pieces[slot, me, :TR, :] = mat[one, cols_of(k + 1)]
+        pieces[slot, me, TR : 2 * TR, :] = mat[one, cols_of(k)]
         pieces[slot, me, 2 * TR :, :] = mat[two, cols_of(k)]
         start_small(k)
 
@@ -372,6 +373,10 @@
         s1 = jnp.clip(PER * (u0 + 2), mid, parts)
         s2 = jnp.clip(PER * (u0 + 3), mid, parts)
 
+        def in_time(j):
+            first = (j + 1) // QS
+            return jnp.minimum(jnp.maximum((j + 1) // WS + 6, PER * (jnp.minimum(first + 1, chunks - 1) + 1)), parts)
+
         def pass_on(slot, a, b):
             def body(w):
                 arrived(slot, w)
@@ -448,12 +453,13 @@
 
         @pl.when(jnp.logical_not(wide))
         def _():
+            sure = jnp.clip(in_time(k - 1), mid, parts)
             finish_pair(major)
-            finish_exchange((mid, parts), (mid, mid))
+            finish_exchange((mid, sure), (mid, mid))
             _half(diag, upper, lower, inv, 0, 16, LANES // 2)
             relay_pair()
             finish_pair(minor)
-            finish_exchange((mid, mid), (mid, parts))
+            finish_exchange((sure, parts), (mid, parts))
             _middle(diag, lower, inv)
 
         @pl.when(jnp.logical_not(wide))
@@ -487,7 +493,7 @@
         over = count - inner
         extra = wide & (over > 0)
         over = jnp.where(extra, over - 1, over)
-        upto = jnp.minimum(jnp.maximum(w0 + 5 + over // 2, PER * (q2 + 1)), parts)
+        upto = jnp.minimum(jnp.maximum(w0 + 6 + over // 2, PER * (q2 + 1)), parts)
         since = jnp.where(k < late, w1 + 1, w0)
         many = jnp.maximum(upto - since, 1)
 
@@ -520,7 +526,7 @@
             for s in range(2):
                 for h in range(2):
                     own_class = pieces.at[now, 2 * (c + 2 * s) + h]
-                    pair[TR * s : TR * s + TR, TC * h : TC * h + TC] = own_class[:TR, :]
+                    pair[TR * s : TR * s + TR, TC * h : TC * h + TC] = own_class[TR : 2 * TR, :]
                     pair[TR * (2 + s) : TR * (2 + s) + TR, TC * h : TC * h + TC] = own_class[2 * TR :, :]
 
         finish_small(k)
@@ -559,6 +565,11 @@
 
         cs = cols_of(k + 1, 2)
         slot = (k + 1) % 3
+
+        u1 = (k + 3) // QS
+        next_mid = jnp.minimum((k + 2) // WS + 1, parts)
+        next_sure = jnp.where(u1 <= wide_u, PER * (u1 + 2), 0)
+        next_sure = jnp.clip(next_sure, next_mid, parts)
 
         def advance(q):
             qa, qb = jnp.minimum(q + 1, chunks - 1), jnp.minimum(q + 2, chunks - 1)
@@ -571,6 +582,10 @@
             yl[rows_of(qa), :] = ya
             xl[rows_of(qb), :] = xb
 
+            @pl.when(major & (k < end - 1) & (q == jnp.maximum(q1, chunks - 2)))
+            def _():
+                pass_on(now, next_mid, next_sure)
+
             for i in range(PER):
                 @pl.when((k < end - 1) & (PER * q + i >= (k + 2) // WS))
                 def _():
@@ -590,13 +605,6 @@
         at = pl.ds(pl.multiple_of(TR * k, TR), TR)
         xl[at, :LANES], xl[at, LANES:] = _own_rows(lower, r)
         each(q0, chunks, lambda q: put(q, k).start())
-
-        u1 = (k + 3) // QS
-        next_mid = jnp.minimum((k + 2) // WS + 1, parts)
-
-        @pl.when(major & (u1 <= wide_u))
-        def _():
-            pass_on(now, next_mid, jnp.clip(PER * (u1 + 2), next_mid, parts))
         return carry
 
     lax.fori_loop(0, end, step, 0)
@@ -611,7 +619,7 @@
     place_next(slot)
     leave(a1, 1).start()
     for i in range(4):
-        s0, s1 = _swap_middle(pieces[slot, 2 * i, TR : 2 * TR, :], pieces[slot, 2 * i + 1, TR : 2 * TR, :])
+        s0, s1 = _swap_middle(pieces[slot, 2 * i, :TR, :], pieces[slot, 2 * i + 1, :TR, :])
         pair[TR * i : TR * i + TR, :LANES] = s0
         pair[TR * i : TR * i + TR, LANES:] = s1
     leave(pair, 2).start()

time: 626 us -> 618 us (0.987)
  Pallas kernels: 625 us -> 618 us
    pallas_call x1, Pallas kernels: 606 us -> 598 us  [local_factor(): pl.pallas_call(lambda *refs: _kernel(steps, *refs), out_shape=(shape, jax...]
where the time goes in v6:
time: 618 us
  Pallas kernels  618 us (100%)
    pallas_call x1, Pallas kernels, local_factor(): pl.pallas_call(lambda *refs: _kernel(steps, *refs), out_shape=(shape, jax...  598 us
    pallas_call x1, Pallas kernels, local_factor(): pl.pallas_call(lambda *refs: _finish(steps, *refs), out_shape=shape, in_s...  19.2 us

profile of v6, /device:TPU:0, one launch (start us, length us, event | category | flops | bytes accessed | tf_op | source)
XLA Modules:
  0.0 617.7 jit_solution(15262277358102524655)
XLA Ops:
  0.0 598.3 %factor.1 = (f32[2048,4096]{1,0:T(8,128)}, f32[3,256,256]{2,1,0:T(8,128)}) custom-call(f32[2048,4096]{1,0:T(8,128)} %bitcast.2), custom_call_target="tpu_custom_call" | custom-call | tf_op jit(solution)/shard_map/factor/pallas_call | solution.py:722
  598.4 19.2 %finish.1 = f32[2048,4096]{1,0:T(8,128)} custom-call(f32[2048,4096]{1,0:T(8,128)} %get-tuple-element.7.refs_0_, f32[3,256,256]{2,1,0:T(8,128)} %get-tuple-element.8.refs_1_), custom_call_target="tpu_custom_call" | custom-call | tf_op jit(solution)/shard_map/finish/pallas_call | solution.py:757

commit v7 on v6

--- a/solution.py
+++ b/solution.py
@@ -16,7 +16,7 @@
 WS = 2
 PER = QS // WS
 LOT = 6
-NARROW = 4
+NARROW = 2
 TILE = 512
 LAST = 2
 ORDER = (0, 2, 1, 3)
@@ -159,7 +159,7 @@
     chunks = steps // QS
     parts = steps // WS
     end = steps - LAST
-    late = steps - 8
+    late = steps - 10
     rows, cols = steps * TR, steps * TC
     tiles = rows // TILE
     wide_u = max(u for u in range(2 * tiles) if sum(tiles - s // 2 for s in range(u, 2 * tiles)) > 4)
@@ -351,7 +351,8 @@
         inner = 0
         for u in range(2 * tiles):
             inner = inner + jnp.where((u >= u0) & (u < u0 + 3), tiles - u // 2, 0)
-        inner = jnp.minimum(inner, 8)
+        rich = (k > 0) & (u0 <= min(1, wide_u - 3))
+        inner = jnp.minimum(inner, jnp.where(rich, 10, 8))
 
         def tile(i, among=count):
             u, past_of, total = 0, 0, 0
@@ -438,8 +439,16 @@
             def half(h):
                 @pl.when(h == 1)
                 def _():
-                    _middle(diag, lower, inv)
                     finish_exchange((s2, parts), (s1, s2))
+
+                    @pl.when(rich)
+                    def _():
+                        tile(8)
+                        _middle(diag, lower, inv)
+
+                    @pl.when(jnp.logical_not(rich))
+                    def _():
+                        _middle(diag, lower, inv)
 
                 for i in range(4):
                     tile(4 * h + i, inner)
@@ -466,7 +475,7 @@
         def _():
             for i in range(NARROW):
                 tile(i)
-            _half(diag, upper, lower, inv, 1, 8, LANES)
+            _half(diag, upper, lower, inv, 1, 16, LANES // 2)
 
         forward_small(k)
 
@@ -478,7 +487,14 @@
 
             each(w0, w1 + 1, body)
 
-        _inverse(lower, inv, invp)
+        @pl.when(rich)
+        def _():
+            tile(9)
+            _inverse(lower, inv, invp)
+
+        @pl.when(jnp.logical_not(rich))
+        def _():
+            _inverse(lower, inv, invp)
 
         @pl.when(wide)
         def _():

time: 618 us -> 617 us (level)
  no operation moved by 1% of the time
where the time goes in v7:
time: 617 us
  Pallas kernels  616 us (100%)
    pallas_call x1, Pallas kernels, local_factor(): pl.pallas_call(lambda *refs: _kernel(steps, *refs), out_shape=(shape, jax...  597 us
    pallas_call x1, Pallas kernels, local_factor(): pl.pallas_call(lambda *refs: _finish(steps, *refs), out_shape=shape, in_s...  19.2 us

profile of v7, /device:TPU:0, one launch (start us, length us, event | category | flops | bytes accessed | tf_op | source)
XLA Modules:
  0.0 616.6 jit_solution(5365445132850148537)
XLA Ops:
  0.0 597.3 %factor.1 = (f32[2048,4096]{1,0:T(8,128)}, f32[3,256,256]{2,1,0:T(8,128)}) custom-call(f32[2048,4096]{1,0:T(8,128)} %bitcast.2), custom_call_target="tpu_custom_call" | custom-call | tf_op jit(solution)/shard_map/factor/pallas_call | solution.py:738
  597.3 19.2 %finish.1 = f32[2048,4096]{1,0:T(8,128)} custom-call(f32[2048,4096]{1,0:T(8,128)} %get-tuple-element.7.refs_0_, f32[3,256,256]{2,1,0:T(8,128)} %get-tuple-element.8.refs_1_), custom_call_target="tpu_custom_call" | custom-call | tf_op jit(solution)/shard_map/finish/pallas_call | solution.py:773
